TPU v7x, 32 devices: a whole 2x2x4 slice. The times are simulated.
32 devices in a mesh: section: 2 (over x), dp: 4 (over z), mp: 4 (over y, core).
Axes of the slice: x: 2, y: 2, z: 4, core: 2. Of those that a mesh axis runs over, the one named last changes fastest.
Arguments:
- text_feats: bfloat16 [4096, 512], P('dp'), may hold values from -48 to 48
- image_feats: bfloat16 [4096, 512], P(('dp', 'mp')), may hold values from -48 to 48
- logit_scale: float32 [1], replicated, may hold values from 10 to 320
- layer_inputs: bfloat16 [2, 4096, 512], P('section', 'dp'), may hold values from -6 to 6
- w_in: bfloat16 [2, 512, 2048], P('section', None, 'mp'), may hold values from -0.25 to 0.25
- w_out: bfloat16 [2, 2048, 512], P('section', 'mp'), may hold values from -0.125 to 0.125
Outputs:
- image_grad: bfloat16 [4096, 512], P(('dp', 'mp'))
- input_grad: bfloat16 [4096, 512], P('dp', 'section')
- w_in_grad: float32 [2, 512, 2048], P('section', 'dp', 'mp')
- w_out_grad_t: float32 [2, 512, 2048], P('section', 'dp', 'mp')
All inputs are finite; a program needn't handle non-finite values.
Results may differ from a plain program's by a relative error of at most 0.017.
Values may be sent and summed in bfloat16 or wider, within the bound.
A program may use at most 128 MiB of HBM per device.

v0:
```python
import jax
import jax.numpy as jnp
from jax import lax
from jax.experimental import pallas as pl
from jax.experimental.pallas import tpu as pltpu
from jax.sharding import PartitionSpec as P

MESH = pl.DeviceIdType.MESH
F32 = jnp.float32
BF16 = jnp.bfloat16
GELU = 1.702
LANES = 128


def unit_rows(values):
    wide = values.astype(F32)
    length = jnp.sqrt(jnp.sum(wide * wide, axis=1, keepdims=True) + 1.0)
    return (wide / length, length)


def unit_backward(unit, length, grad_unit):
    return (grad_unit - unit * jnp.sum(unit * grad_unit, axis=1, keepdims=True)) / length


def dot_nn(a, b):
    return lax.dot_general(a, b, (((1,), (0,)), ((), ())), preferred_element_type=F32)


def dot_nt(a, b):
    return lax.dot_general(a, b, (((1,), (1,)), ((), ())), preferred_element_type=F32)


def dot_tn(a, b):
    return lax.dot_general(a, b, (((0,), (0,)), ((), ())), preferred_element_type=F32)


def tile(index, size):
    return pl.ds(pl.multiple_of(index * size, size), size)


def make_kernel(n_sec, n_dp, n_mp):
    cores = 2 if n_mp % 2 == 0 else 1
    chips = n_mp // cores

    def kernel(
        text, image, scale_ref, hidden, w_in, w_out,
        image_out, input_out, first_out, second_out,
        text_low, cols, scores, sgrad, row_max, row_lse, row_st, row_rx, col_st, col_rx,
        wi_all, wo_all, t_tx, t_rx, t_own, g_all, g_acc, g_new, act_all, pre_all,
        w_tx, w_rx, i_tx, i_rx,
        gat_s, gat_r, fwd_s, fwd_r, cs_s, cs_r, rs_s, rs_r, wi_s, wi_r, wo_s, wo_r,
        t_s, t_r, g_s, g_r, x_s, x_r, in_s, in_r, ix_s, ix_r, w_s, w_r, im_s, im_r, io_s, io_r,
    ):
        s = lax.axis_index("section")
        d = lax.axis_index("dp")
        m = lax.axis_index("mp")
        last = n_sec - 1
        rows = text.shape[0]
        own = image.shape[0]
        half = own // n_sec
        quarter = rows // n_mp
        feats = text.shape[1]
        share = feats // n_dp
        width = feats // n_sec
        mult = scale_ref[0]
        core = lax.rem(m, cores)
        chip = m // cores

        def copy(src, dst, send, recv, where):
            return pltpu.make_async_remote_copy(
                src_ref=src, dst_ref=dst, send_sem=send, recv_sem=recv,
                device_id=where, device_id_type=MESH,
            )

        def others(mine, count):
            return [lax.rem(mine + k, count) for k in range(1, count)]

        def sources(mine, count):
            return [lax.rem(mine + count - k, count) for k in range(1, count)]

        barrier = pltpu.get_barrier_semaphore()
        for p in others(d, n_dp):
            pl.semaphore_signal(barrier, inc=1, device_id={"dp": p}, device_id_type=MESH)
        for p in others(m, n_mp):
            pl.semaphore_signal(barrier, inc=1, device_id={"mp": p}, device_id_type=MESH)
        for p in others(s, n_sec):
            pl.semaphore_signal(barrier, inc=1, device_id={"section": p}, device_id_type=MESH)

        own_unit, _ = unit_rows(image[...])
        cols[tile(d, own), :] = own_unit.astype(BF16)
        pl.semaphore_wait(barrier, n_dp + n_mp + n_sec - 3)

        def cut(block, sec):
            return cols.at[pl.ds(pl.multiple_of(block * own + sec * half, half), half), :]

        gathers = []
        for p in others(d, n_dp):
            c = copy(cut(d, s), cut(d, s), gat_s.at[p], gat_r.at[d], {"dp": p})
            c.start()
            gathers.append(c)

        class Spread:
            def __init__(self, slot, send, recv):
                self.slot, self.send, self.recv = slot, send, recv
                self.sent = []

            def push(self, index, to):
                c = copy(self.slot(index), self.slot(index), self.send.at[len(self.sent)],
                         self.recv.at[index], {"mp": to})
                c.start()
                self.sent.append(c)

            def arrived(self, index):
                copy(self.slot(index), self.slot(index), self.send.at[0],
                     self.recv.at[index], {"mp": lax.rem(m + 1, n_mp)}).wait_recv()

            def start(self):
                for q in others(chip, chips):
                    self.push(m, q * cores + core)
                for e in others(core, cores):
                    self.push(m, chip * cores + e)

            def relay(self):
                for q in sources(chip, chips):
                    index = q * cores + core
                    self.arrived(index)
                    for e in others(core, cores):
                        self.push(index, chip * cores + e)

            def finish(self):
                for e in sources(core, cores):
                    self.arrived(chip * cores + e)
                    for q in sources(chip, chips):
                        self.arrived(q * cores + e)

            def drain(self):
                for c in self.sent:
                    c.wait_send()

        wi_all[m] = w_in[...]
        wo_all[m] = w_out[...]
        wi_spread = Spread(lambda k: wi_all.at[k], wi_s, wi_r)
        wo_spread = Spread(lambda k: wo_all.at[k], wo_s, wo_r)
        wi_spread.start()
        wo_spread.start()

        @pl.loop(0, n_mp)
        def _(r):
            unit, _ = unit_rows(text[tile(r, quarter), :])
            text_low[tile(r, quarter), :] = unit.astype(BF16)

        row_max[...] = jnp.full(row_max.shape, -1e30, F32)

        def block_scores(p):
            piece = cols[tile(p, own), :]

            def chunk(r, peak):
                value = mult * dot_nt(text_low[tile(r, quarter), :], piece)
                scores[tile(r, quarter), tile(p, own)] = value
                best = row_max[tile(r, quarter), :]
                for k in range(0, own, LANES):
                    best = jnp.maximum(best, value[:, k : k + LANES])
                row_max[tile(r, quarter), :] = best
                return jnp.maximum(peak, jnp.max(value, axis=0, keepdims=True))

            peak = lax.fori_loop(0, n_mp, chunk, jnp.full((1, own), -1e30, F32))

            def total(r, acc):
                value = scores[tile(r, quarter), tile(p, own)]
                return acc + jnp.sum(jnp.exp(value - peak), axis=0, keepdims=True)

            acc = lax.fori_loop(0, n_mp, total, jnp.zeros((1, own), F32))
            col_st[pl.ds(p, 1), :] = peak
            col_st[pl.ds(n_dp + p, 1), :] = acc

        block_scores(d)
        forwards = []
        for k, p in enumerate(sources(d, n_dp)):
            copy(cut(p, s), cut(p, s), gat_s.at[p], gat_r.at[p], {"dp": p}).wait_recv()
            for t in others(s, n_sec):
                c = copy(cut(p, s), cut(p, s), fwd_s.at[t, p], fwd_r.at[s, p], {"section": t})
                c.start()
                forwards.append(c)
        for p in sources(d, n_dp):
            for t in sources(s, n_sec):
                copy(cut(p, t), cut(p, t), fwd_s.at[t, p], fwd_r.at[t, p],
                     {"section": t}).wait_recv()
            block_scores(p)

        col_rx[d] = col_st[...]
        col_sent = []
        for p in others(d, n_dp):
            c = copy(col_st, col_rx.at[d], cs_s.at[p], cs_r.at[d], {"dp": p})
            c.start()
            col_sent.append(c)

        for r in range(n_mp):
            part = pl.ds(r * quarter, quarter)
            peak = jnp.max(row_max[part, :], axis=1, keepdims=True)

            def total(p, acc):
                value = jnp.exp(scores[part, tile(p, own)] - peak)
                for k in range(0, own, LANES):
                    acc = acc + value[:, k : k + LANES]
                return acc

            acc = lax.fori_loop(0, n_dp, total, jnp.zeros((quarter, LANES), F32))
            acc = jnp.sum(acc, axis=1, keepdims=True)
            wide_peak = jnp.broadcast_to(peak, (quarter, LANES)).T
            wide_sum = jnp.broadcast_to(acc, (quarter, LANES)).T
            row_st[r : r + 1, :] = wide_peak[0:1, :]
            row_st[n_mp + r : n_mp + r + 1, :] = wide_sum[0:1, :]

        row_rx[m] = row_st[...]
        row_sent = []
        for p in others(m, n_mp):
            c = copy(row_st, row_rx.at[m], rs_s.at[p], rs_r.at[m], {"mp": p})
            c.start()
            row_sent.append(c)

        def merge(rx, count, n):
            peak = rx[0, 0:n, :]
            for k in range(1, count):
                peak = jnp.maximum(peak, rx[k, 0:n, :])
            acc = jnp.zeros(peak.shape, F32)
            for k in range(count):
                acc = acc + rx[k, n : 2 * n, :] * jnp.exp(rx[k, 0:n, :] - peak)
            return peak + jnp.log(acc)

        for p in sources(d, n_dp):
            copy(col_st, col_rx.at[p], cs_s.at[p], cs_r.at[p], {"dp": p}).wait_recv()
        col_lse = merge(col_rx, n_dp, n_dp)
        col_st_rows = [col_lse[k : k + 1, :] for k in range(n_dp)]
        for p in sources(m, n_mp):
            copy(row_st, row_rx.at[p], rs_s.at[p], rs_r.at[p], {"mp": p}).wait_recv()
        merged = merge(row_rx, n_mp, n_mp)
        for r in range(n_mp):
            row_lse[r] = jnp.broadcast_to(merged[r : r + 1, :], (LANES, quarter)).T

        def score_rows(r):
            line = row_lse[r]
            text_id = lax.broadcasted_iota(jnp.int32, (quarter, LANES), 0) + d * rows + r * quarter
            for p in range(n_dp):
                for k in range(0, own, LANES):
                    value = scores[tile(r, quarter), p * own + k : p * own + k + LANES]
                    both = jnp.exp(value - line) + jnp.exp(value - col_st_rows[p][:, k : k + LANES])
                    image_id = lax.broadcasted_iota(jnp.int32, (quarter, LANES), 1) + (
                        (p * n_mp + m) * own + k
                    )
                    out = 0.5 * both - jnp.where(text_id == image_id, 1.0, 0.0)
                    sgrad[tile(r, quarter), p * own + k : p * own + k + LANES] = out.astype(BF16)

        @pl.loop(0, n_mp)
        def _(k):
            r = lax.rem(m + 1 + k, n_mp)
            score_rows(r)

            @pl.when(s == last)
            def _():
                value = dot_nn(sgrad[tile(r, quarter), :], cols[...])

                @pl.when(k < n_mp - 1)
                def _():
                    t_tx[r] = value.astype(BF16)
                    copy(t_tx.at[r], t_rx.at[m], t_s.at[r], t_r.at[m], {"mp": r}).start()

                @pl.when(k == n_mp - 1)
                def _():
                    t_own[...] = value

        def image_part(p):
            at = pl.ds(pl.multiple_of(p * own + s * half, half), half)
            return dot_tn(sgrad[:, at], text_low[...])

        image_sent = []
        for p in others(d, n_dp):
            i_tx[p] = image_part(p).astype(BF16)
            c = copy(i_tx.at[p], i_rx.at[d], im_s.at[p], im_r.at[d], {"dp": p})
            c.start()
            image_sent.append(c)

        wi_spread.relay()
        wo_spread.relay()

        mine = tile(m, quarter)

        @pl.when(s == last)
        def _():
            total = t_own[...]
            for p in sources(m, n_mp):
                copy(t_tx.at[p], t_rx.at[p], t_s.at[p], t_r.at[p], {"mp": p}).wait_recv()
                total = total + t_rx[p].astype(F32)
            unit, length = unit_rows(text[mine, :])
            g_all[m] = unit_backward(unit, length, mult * total).astype(BF16)

        wi_spread.finish()
        wo_spread.finish()

        @pl.when(s != last)
        def _():
            copy(g_new, g_all.at[m], x_s, x_r, {"section": s + 1}).wait_recv()

        g_spread = Spread(lambda k: g_all.at[k], g_s, g_r)
        g_spread.start()

        def slopes(pre, back):
            sigm = 1.0 / (1.0 + jnp.exp(-GELU * pre))
            grad = back * (sigm + GELU * pre * sigm * (1.0 - sigm))
            return (pre * sigm).astype(BF16), grad.astype(BF16)

        g_acc[...] = g_all[m].astype(F32)

        @pl.loop(0, n_mp)
        def _(j):
            pre = dot_nn(hidden[mine, :], wi_all[j])
            back = dot_nt(g_all[m], wo_all[j])
            _, grad = slopes(pre, back)
            g_acc[...] += dot_nt(grad, wi_all[j])

        g_new[...] = g_acc[...].astype(BF16)

        @pl.when(s > 0)
        def _():
            copy(g_new, g_all.at[m], x_s, x_r, {"section": s - 1}).start()

        def slab(k):
            return input_out.at[tile(k, quarter), :]

        def final(t):
            return copy(g_new.at[:, t * width : (t + 1) * width], slab(m), ix_s.at[t], ix_r,
                        {"section": t})

        @pl.when(s == 0)
        def _():
            for t in range(1, n_sec):
                final(t).start()
            input_out[mine, :] = g_new[:, 0:width]

        g_spread.relay()
        g_spread.finish()
        in_spread = Spread(slab, in_s, in_r)

        @pl.loop(0, n_mp)
        def _(r):
            pre = dot_nn(hidden[tile(r, quarter), :], w_in[...])
            back = dot_nt(g_all[r], w_out[...])
            act, grad = slopes(pre, back)
            act_all[tile(r, quarter), :] = act
            pre_all[tile(r, quarter), :] = grad

        g_rows = g_all[...].reshape(rows, feats)
        grad_second = dot_tn(g_rows, act_all[...])
        for p in range(n_dp):
            w_tx[p, 1] = grad_second[p * share : (p + 1) * share, :].astype(BF16)
        weight_sent = []

        def send_weights(which):
            for p in others(d, n_dp):
                c = copy(w_tx.at[p, which], w_rx.at[d, which], w_s.at[which, p],
                         w_r.at[which, d], {"dp": p})
                c.start()
                weight_sent.append(c)

        send_weights(1)
        grad_first = dot_tn(hidden[...], pre_all[...])
        for p in range(n_dp):
            w_tx[p, 0] = grad_first[p * share : (p + 1) * share, :].astype(BF16)
        send_weights(0)

        @pl.when(s != 0)
        def _():
            copy(g_new.at[:, 0:width], slab(m), ix_s.at[0], ix_r, {"section": 0}).wait_recv()

        in_spread.start()

        image_half = pl.ds(pl.multiple_of(s * half, half), half)
        total = image_part(d)
        for p in sources(d, n_dp):
            copy(i_tx.at[p], i_rx.at[p], im_s.at[p], im_r.at[p], {"dp": p}).wait_recv()
            total = total + i_rx[p].astype(F32)
        unit, length = unit_rows(image[image_half, :])
        image_out[image_half, :] = unit_backward(unit, length, mult * total).astype(BF16)
        out_sent = []
        for t in others(s, n_sec):
            c = copy(image_out.at[image_half, :], image_out.at[image_half, :],
                     io_s.at[t], io_r.at[s], {"section": t})
            c.start()
            out_sent.append(c)

        in_spread.relay()
        in_spread.finish()

        for which, out in ((1, second_out), (0, first_out)):
            total = w_tx[d, which].astype(F32)
            for p in sources(d, n_dp):
                copy(w_tx.at[p, which], w_rx.at[p, which], w_s.at[which, p],
                     w_r.at[which, p], {"dp": p}).wait_recv()
                total = total + w_rx[p, which].astype(F32)
            out[...] = total

        for t in sources(s, n_sec):
            part = image_out.at[pl.ds(pl.multiple_of(t * half, half), half), :]
            copy(part, part, io_s.at[t], io_r.at[t], {"section": t}).wait_recv()

        for c in gathers + forwards + col_sent + row_sent + image_sent + weight_sent + out_sent:
            c.wait_send()
        for spread in (wi_spread, wo_spread, g_spread, in_spread):
            spread.drain()

        @pl.when(s == last)
        def _():
            for p in others(m, n_mp):
                copy(t_tx.at[p], t_rx.at[m], t_s.at[p], t_r.at[m], {"mp": p}).wait_send()

        @pl.when(s > 0)
        def _():
            copy(g_new, g_all.at[m], x_s, x_r, {"section": s - 1}).wait_send()

        @pl.when(s == 0)
        def _():
            for t in range(1, n_sec):
                final(t).wait_send()

    return kernel


def solution(mesh):
    n_sec, n_dp, n_mp = mesh.shape["section"], mesh.shape["dp"], mesh.shape["mp"]

    def body(text, image, scale, hidden, w_in, w_out):
        rows, feats = text.shape
        own = image.shape[0]
        hid = w_in.shape[2]
        quarter, half, share = rows // n_mp, own // n_sec, feats // n_dp
        columns = own * n_dp
        dma = pltpu.SemaphoreType.DMA
        vmem = pl.BlockSpec(memory_space=pltpu.VMEM)
        out = pl.pallas_call(
            make_kernel(n_sec, n_dp, n_mp),
            out_shape=(
                jax.ShapeDtypeStruct((own, feats), BF16),
                jax.ShapeDtypeStruct((rows, feats // n_sec), BF16),
                jax.ShapeDtypeStruct((share, hid), F32),
                jax.ShapeDtypeStruct((share, hid), F32),
            ),
            in_specs=[vmem, vmem, pl.BlockSpec(memory_space=pltpu.SMEM), vmem, vmem, vmem],
            out_specs=(vmem,) * 4,
            scratch_shapes=[
                pltpu.VMEM((rows, feats), BF16),
                pltpu.VMEM((columns, feats), BF16),
                pltpu.VMEM((rows, columns), F32),
                pltpu.VMEM((rows, columns), BF16),
                pltpu.VMEM((rows, LANES), F32),
                pltpu.VMEM((n_mp, quarter, LANES), F32),
                pltpu.VMEM((2 * n_mp, quarter), F32),
                pltpu.VMEM((n_mp, 2 * n_mp, quarter), F32),
                pltpu.VMEM((2 * n_dp, own), F32),
                pltpu.VMEM((n_dp, 2 * n_dp, own), F32),
                pltpu.VMEM((n_mp, feats, hid), BF16),
                pltpu.VMEM((n_mp, hid, feats), BF16),
                pltpu.VMEM((n_mp, quarter, feats), BF16),
                pltpu.VMEM((n_mp, quarter, feats), BF16),
                pltpu.VMEM((quarter, feats), F32),
                pltpu.VMEM((n_mp, quarter, feats), BF16),
                pltpu.VMEM((quarter, feats), F32),
                pltpu.VMEM((quarter, feats), BF16),
                pltpu.VMEM((rows, hid), BF16),
                pltpu.VMEM((rows, hid), BF16),
                pltpu.VMEM((n_dp, 2, share, hid), BF16),
                pltpu.VMEM((n_dp, 2, share, hid), BF16),
                pltpu.VMEM((n_dp, half, feats), BF16),
                pltpu.VMEM((n_dp, half, feats), BF16),
                dma((n_dp,)), dma((n_dp,)),
                dma((n_sec, n_dp)), dma((n_sec, n_dp)),
                dma((n_dp,)), dma((n_dp,)),
                dma((n_mp,)), dma((n_mp,)),
                dma((2 * n_mp,)), dma((n_mp,)),
                dma((2 * n_mp,)), dma((n_mp,)),
                dma((n_mp,)), dma((n_mp,)),
                dma((2 * n_mp,)), dma((n_mp,)),
                dma, dma,
                dma((2 * n_mp,)), dma((n_mp,)),
                dma((n_sec,)), dma,
                dma((2, n_dp)), dma((2, n_dp)),
                dma((n_dp,)), dma((n_dp,)),
                dma((n_sec,)), dma((n_sec,)),
            ],
            compiler_params=pltpu.CompilerParams(
                collective_id=0, has_side_effects=True, vmem_limit_bytes=63000000
            ),
        )(text, image, scale, hidden[0], w_in[0], w_out[0])
        image_grad, input_grad, first, second = out
        return (image_grad, input_grad, first[None], second[None])

    return jax.shard_map(
        body,
        mesh=mesh,
        in_specs=(
            P("dp", None),
            P(("dp", "mp"), None),
            P(),
            P("section", "dp", None),
            P("section", None, "mp"),
            P("section", "mp", None),
        ),
        out_specs=(
            P(("dp", "mp"), None),
            P("dp", "section"),
            P("section", "dp", "mp"),
            P("section", "dp", "mp"),
        ),
        check_vma=False,
    )
```

profile of v0, /device:TPU:0, one launch (start us, length us, event | category | flops | bytes accessed | tf_op | source)
XLA Modules:
  0.0 92.5 jit_solution(4735918846649673005)
XLA Ops:
  1.3 86.6 %shard_map.93 = (bf16[256,512]{1,0:T(8,128)(2,1)}, bf16[1024,256]{1,0:T(8,128)(2,1)}, f32[128,512]{1,0:T(8,128)}, f32[128,512]{1,0:T(8,128)}) custom-call(bf16[1024,512]{1,0:T(8,128)(2,1)} %text.1, bf16[256,512]{1,0:T(8,128)(2,1)} %image.1, f32[1]{0:T(128)S(6)} %copy.14.scale_ref, bf16[1024,512]{1,0:T(8,128)(2,1)} %bitcast.5, bf16[512,512]{1,0:T(8,128)(2,1)} %bitcast.6, ...), custom_call_target="tpu_custom_call" | custom-call | tf_op jit(solution)/shard_map/pallas_call | solution.py:438
  87.9 0.0 copy-start
  87.9 1.7 %copy.15 = bf16[256,512]{1,0:T(8,128)(2,1)} copy(bf16[256,512]{1,0:T(8,128)(2,1)} %get-tuple-element.16) | data formatting | bytes 524288
  89.6 0.0 copy-done
  89.6 0.0 copy-start.2
  89.6 0.8 copy.16
  90.4 0.3 copy-done.2
  90.7 0.0 copy-start.1
  90.7 0.7 copy.17
  91.4 0.3 copy-done.1
  91.8 0.7 copy.18
Async XLA Ops:
  87.9 1.7 %copy-start = (bf16[1024,256]{1,0:T(8,128)(2,1)S(1)}, bf16[1024,256]{1,0:T(8,128)(2,1)}, u32[]{:S(2)}) copy-start(bf16[1024,256]{1,0:T(8,128)(2,1)} %get-tuple-element.17) | copy-start | bytes 1572868
  89.6 1.1 %copy-start.2 = (f32[128,512]{1,0:T(8,128)S(1)}, f32[128,512]{1,0:T(8,128)}, u32[]{:S(2)}) copy-start(f32[128,512]{1,0:T(8,128)} %get-tuple-element.10) | copy-start | bytes 786436
  90.7 1.0 %copy-start.1 = (f32[128,512]{1,0:T(8,128)S(1)}, f32[128,512]{1,0:T(8,128)}, u32[]{:S(2)}) copy-start(f32[128,512]{1,0:T(8,128)} %get-tuple-element.11) | copy-start | bytes 786436
where the time goes:
time: 92.7 us; the launch traced here: 92.5 us
  Pallas kernels  86.6 us (93%)
  local copies, waits for them, and re-layouts  4.57 us (5%)
  between operations  1.3 us (1%)
    pallas_call x1, Pallas kernels, body(): pl.pallas_call(make_kernel(n_sec, n_dp, n_mp), out_shape=(jax.ShapeDtypeS...  86.6 us
    unnamed x10, local copies, waits for them, and re-layouts  4.57 us

commit v1 on v0

v1 whole, which is shorter than its diff:
```python
import jax
import jax.numpy as jnp
from jax import lax
from jax.experimental import pallas as pl
from jax.experimental.pallas import tpu as pltpu
from jax.sharding import PartitionSpec as P

MESH = pl.DeviceIdType.MESH
F32 = jnp.float32
BF16 = jnp.bfloat16
GELU = 1.702
LANES = 128
PIECES = 4


def unit_rows(values):
    wide = values.astype(F32)
    length = jnp.sqrt(jnp.sum(wide * wide, axis=1, keepdims=True) + 1.0)
    return (wide / length, length)


def unit_backward(unit, length, grad_unit):
    return (grad_unit - unit * jnp.sum(unit * grad_unit, axis=1, keepdims=True)) / length


def dot_nn(a, b):
    return lax.dot_general(a, b, (((1,), (0,)), ((), ())), preferred_element_type=F32)


def dot_nt(a, b):
    return lax.dot_general(a, b, (((1,), (1,)), ((), ())), preferred_element_type=F32)


def dot_tn(a, b):
    return lax.dot_general(a, b, (((0,), (0,)), ((), ())), preferred_element_type=F32)


def tile(index, size):
    return pl.ds(pl.multiple_of(index * size, size), size)


def pick(index, values):
    out = 0
    for k, v in enumerate(values):
        out = out + jnp.where(index == k, v, 0)
    return out


def nearest(count):
    return [sorted((p for p in range(count) if p != i), key=lambda p: (abs(p - i), p)) for i in range(count)]


def make_kernel(n_sec, n_dp, n_mp):
    cores = 2 if n_mp % 2 == 0 else 1
    chips = n_mp // cores

    def kernel(
        text_in, image_in, scale_ref, hidden_in, w_in, w_out,
        image_out, input_out, first_out, second_out,
        text, image, hidden,
        text_low, cols, scores, sgrad, row_max, row_lse, row_st, row_rx, col_st, col_rx,
        wi_all, wo_all, slope_own, slope_all, act_all, pre_all,
        a_tx, a_rx, b_tx, b_rx, c_tx, c_rx, t_acc, g_all, g_new,
        w_tx, w_rx, i_tx, i_rx,
        ld, gat_s, gat_r, cs_s, cs_r, rs_s, rs_r, wi_s, wi_r, wo_s, wo_r,
        a_s, a_r, b_s, b_r, c_s, c_r, g_s, g_r, x_s, x_r, in_s, in_r, ix_s, ix_r,
        w_s, w_r, im_s, im_r, io_s, io_r,
    ):
        s = lax.axis_index("section")
        d = lax.axis_index("dp")
        m = lax.axis_index("mp")
        last = n_sec - 1
        rows, feats = text.shape
        own = image.shape[0]
        half = own // n_sec
        quarter = rows // n_mp
        piece = quarter // PIECES
        hid = slope_all.shape[1]
        share = feats // n_dp
        width = feats // n_sec
        mult = scale_ref[0]
        core = lax.rem(m, cores)
        chip = m // cores

        def copy(src, dst, send, recv, where):
            return pltpu.make_async_remote_copy(
                src_ref=src, dst_ref=dst, send_sem=send, recv_sem=recv,
                device_id=where, device_id_type=MESH,
            )

        def others(mine, count):
            return [lax.rem(mine + k, count) for k in range(1, count)]

        def sources(mine, count):
            return [lax.rem(mine + count - k, count) for k in range(1, count)]

        order = nearest(n_dp)
        near = [pick(d, [order[i][k] for i in range(n_dp)]) for k in range(n_dp - 1)]
        far = near[::-1]

        barrier = pltpu.get_barrier_semaphore()
        plane = [(t, p) for t in [s] + others(s, n_sec) for p in [m] + others(m, n_mp)][1:]
        for t, p in plane:
            pl.semaphore_signal(barrier, inc=1, device_id={"section": t, "mp": p}, device_id_type=MESH)
        for p in near:
            pl.semaphore_signal(barrier, inc=1, device_id={"dp": p}, device_id_type=MESH)

        loads = [
            pltpu.make_async_copy(image_in, image, ld.at[0]),
            pltpu.make_async_copy(w_in, wi_all.at[m], ld.at[1]),
            pltpu.make_async_copy(w_out, wo_all.at[m], ld.at[2]),
            pltpu.make_async_copy(text_in, text, ld.at[3]),
            pltpu.make_async_copy(hidden_in, hidden, ld.at[4]),
        ]
        for c in loads:
            c.start()

        mine_half = tile(s, half)
        loads[0].wait()
        own_unit, _ = unit_rows(image[mine_half, :])
        cols[tile(d, half), :] = own_unit.astype(BF16)
        loads[1].wait()
        loads[2].wait()
        pl.semaphore_wait(barrier, len(plane) + n_dp - 1)

        gathers = []
        for p in far:
            c = copy(cols.at[tile(d, half), :], cols.at[tile(d, half), :], gat_s.at[p], gat_r.at[d], {"dp": p})
            c.start()
            gathers.append(c)

        class Spread:
            def __init__(self, slot, send, recv):
                self.slot, self.send, self.recv = slot, send, recv
                self.sent = []

            def push(self, index, to):
                c = copy(self.slot(index), self.slot(index), self.send.at[len(self.sent)],
                         self.recv.at[index], {"mp": to})
                c.start()
                self.sent.append(c)

            def arrived(self, index):
                copy(self.slot(index), self.slot(index), self.send.at[0],
                     self.recv.at[index], {"mp": lax.rem(m + 1, n_mp)}).wait_recv()

            def start(self):
                for q in others(chip, chips):
                    self.push(m, q * cores + core)
                for e in others(core, cores):
                    self.push(m, chip * cores + e)

            def relay(self):
                for q in sources(chip, chips):
                    index = q * cores + core
                    self.arrived(index)
                    for e in others(core, cores):
                        self.push(index, chip * cores + e)

            def finish(self):
                for e in sources(core, cores):
                    self.arrived(chip * cores + e)
                    for q in sources(chip, chips):
                        self.arrived(q * cores + e)

            def drain(self):
                for c in self.sent:
                    c.wait_send()

        def cut(ref, n, k):
            size = ref.shape[1] // n
            return lambda j: ref.at[j, k * size : (k + 1) * size, :]

        wi_spread = Spread(cut(wi_all, 1, 0), wi_s, wi_r)
        wo_spread = [Spread(cut(wo_all, 2, k), wo_s.at[k], wo_r.at[k]) for k in range(2)]
        wi_spread.start()

        loads[3].wait()

        @pl.loop(0, n_mp)
        def _(r):
            unit, _ = unit_rows(text[tile(r, quarter), :])
            text_low[tile(r, quarter), :] = unit.astype(BF16)

        row_max[...] = jnp.full(row_max.shape, -1e30, F32)

        def block_scores(p):
            block = cols[tile(p, half), :]
            peak = jnp.full((1, half), -1e30, F32)
            for r in range(n_mp):
                part = pl.ds(r * quarter, quarter)
                value = mult * dot_nt(text_low[part, :], block)
                scores[part, tile(p, half)] = value
                best = row_max[part, :]
                for k in range(0, half, LANES):
                    best = jnp.maximum(best, value[:, k : k + LANES])
                row_max[part, :] = best
                peak = jnp.maximum(peak, jnp.max(value, axis=0, keepdims=True))
            acc = jnp.zeros((1, half), F32)
            for r in range(n_mp):
                value = scores[pl.ds(r * quarter, quarter), tile(p, half)]
                acc = acc + jnp.sum(jnp.exp(value - peak), axis=0, keepdims=True)
            col_st[pl.ds(p, 1), :] = peak
            col_st[pl.ds(n_dp + p, 1), :] = acc

        block_scores(d)

        def gelu_terms(pre):
            sigm = 1.0 / (1.0 + jnp.exp(-GELU * pre))
            return pre * sigm, sigm + GELU * pre * sigm * (1.0 - sigm)

        loads[4].wait()

        @pl.loop(0, n_mp)
        def _(r):
            act, slope = gelu_terms(dot_nn(hidden[tile(r, quarter), :], wi_all[m]))
            act_all[tile(r, quarter), :] = act.astype(BF16)
            slope_all[tile(r, quarter), :] = slope

        @pl.loop(0, n_dp - 1)
        def _(k):
            p = near[0]
            for i in range(1, n_dp - 1):
                p = jnp.where(k == i, near[i], p)
            copy(cols.at[tile(p, half), :], cols.at[tile(p, half), :], gat_s.at[p], gat_r.at[p], {"dp": p}).wait_recv()
            block_scores(p)

        col_rx[d] = col_st[...]
        col_sent = []
        for p in far:
            c = copy(col_st, col_rx.at[d], cs_s.at[p], cs_r.at[d], {"dp": p})
            c.start()
            col_sent.append(c)

        for r in range(n_mp):
            part = pl.ds(r * quarter, quarter)
            peak = jnp.max(row_max[part, :], axis=1, keepdims=True)
            acc = jnp.zeros((quarter, LANES), F32)
            for k in range(0, n_dp * half, LANES):
                acc = acc + jnp.exp(scores[part, k : k + LANES] - peak)
            acc = jnp.sum(acc, axis=1, keepdims=True)
            wide_peak = jnp.broadcast_to(peak, (quarter, LANES)).T
            wide_sum = jnp.broadcast_to(acc, (quarter, LANES)).T
            row_st[r : r + 1, :] = wide_peak[0:1, :]
            row_st[n_mp + r : n_mp + r + 1, :] = wide_sum[0:1, :]

        here = s * n_mp + m
        row_rx[here] = row_st[...]
        row_sent = []
        for k, (t, p) in enumerate(plane):
            c = copy(row_st, row_rx.at[here], rs_s.at[k], rs_r.at[here], {"section": t, "mp": p})
            c.start()
            row_sent.append(c)

        wo_spread[0].start()

        def merge(rx, count, n):
            peak = rx[0, 0:n, :]
            for k in range(1, count):
                peak = jnp.maximum(peak, rx[k, 0:n, :])
            acc = jnp.zeros(peak.shape, F32)
            for k in range(count):
                acc = acc + rx[k, n : 2 * n, :] * jnp.exp(rx[k, 0:n, :] - peak)
            return peak + jnp.log(acc)

        for p in near:
            copy(col_st, col_rx.at[p], cs_s.at[p], cs_r.at[p], {"dp": p}).wait_recv()
        col_lse = merge(col_rx, n_dp, n_dp)
        for t, p in plane:
            copy(row_st, row_rx.at[t * n_mp + p], rs_s.at[0], rs_r.at[t * n_mp + p],
                 {"section": t, "mp": p}).wait_recv()
        merged = merge(row_rx, n_sec * n_mp, n_mp)
        for r in range(n_mp):
            row_lse[r] = jnp.broadcast_to(merged[r : r + 1, :], (LANES, quarter)).T

        def score_rows(r):
            line = row_lse[r]
            for p in range(n_dp):
                for k in range(0, half, LANES):
                    at = pl.ds(p * half + k, LANES)
                    value = scores[tile(r, quarter), at]
                    both = jnp.exp(value - line) + jnp.exp(value - col_lse[p : p + 1, k : k + LANES])
                    sgrad[tile(r, quarter), at] = (0.5 * both).astype(BF16)

        def score_diagonal():
            line = row_lse[m]
            text_id = lax.broadcasted_iota(jnp.int32, (quarter, LANES), 0)
            lse = col_lse[0:1, :]
            for p in range(1, n_dp):
                lse = jnp.where(d == p, col_lse[p : p + 1, :], lse)
            for k in range(0, half, LANES):
                at = pl.ds(pl.multiple_of(d * half + k, LANES), LANES)
                value = scores[tile(m, quarter), at]
                both = jnp.exp(value - line) + jnp.exp(value - lse[:, k : k + LANES])
                image_id = lax.broadcasted_iota(jnp.int32, (quarter, LANES), 1) + (s * half + k)
                out = 0.5 * both - jnp.where(text_id == image_id, 1.0, 0.0)
                sgrad[tile(m, quarter), at] = out.astype(BF16)

        def text_part(r):
            return dot_nn(sgrad[tile(r, quarter), :], cols[...])

        def rows_of(k):
            return tile(k, piece)

        a_sent, b_sent = [], []

        def for_sibling(q):
            for e in others(core, cores):
                r = q * cores + e
                score_rows(r)
                a_tx[q] = text_part(r).astype(BF16)
                c = copy(a_tx.at[q], a_rx.at[q], a_s.at[q], a_r.at[q], {"mp": chip * cores + e})
                c.start()
                a_sent.append(c)

        def from_sibling(q):
            for e in others(core, cores):
                copy(a_tx.at[q], a_rx.at[q], a_s.at[q], a_r.at[q], {"mp": chip * cores + e}).wait_recv()
                t_acc[...] += a_rx[q].astype(F32)

        for q in others(chip, chips):
            for_sibling(q)
            score_rows(q * cores + core)
            t_acc[...] = text_part(q * cores + core)
            from_sibling(q)
            b_tx[q] = t_acc[...].astype(BF16)
            for k in range(PIECES):
                c = copy(b_tx.at[q, rows_of(k), :], b_rx.at[chip, rows_of(k), :], b_s.at[q, k], b_r.at[chip, k],
                         {"mp": q * cores + core})
                c.start()
                b_sent.append(c)
        wo_spread[1].start()
        for_sibling(chip)
        score_rows(m)
        score_diagonal()
        t_acc[...] = text_part(m)

        def image_part(p):
            return dot_tn(sgrad[:, tile(p, half)], text_low[...])

        image_sent = []
        for p in far:
            i_tx[p] = image_part(p).astype(BF16)
            c = copy(i_tx.at[p], i_rx.at[d], im_s.at[p], im_r.at[d], {"dp": p})
            c.start()
            image_sent.append(c)
        i_tx[d] = image_part(d).astype(BF16)

        from_sibling(chip)
        wi_spread.relay()
        wi_spread.finish()
        mine = tile(m, quarter)

        @pl.loop(0, n_mp)
        def _(j):
            _, slope = gelu_terms(dot_nn(hidden[mine, :], wi_all[j]))
            slope_own[j] = slope

        wo_spread[0].relay()

        def gather_sum(k):
            total = t_acc[rows_of(k), :]
            for q in sources(chip, chips):
                copy(b_tx.at[q, rows_of(k), :], b_rx.at[q, rows_of(k), :], b_s.at[q, k], b_r.at[q, k],
                     {"mp": q * cores + core}).wait_recv()
                total = total + b_rx[q, rows_of(k), :].astype(F32)
            return total

        def to_last(k):
            return copy(c_tx.at[rows_of(k), :], c_rx.at[s, rows_of(k), :], c_s.at[k], c_r.at[s, k],
                        {"section": last})

        def to_below(k):
            return copy(g_new.at[rows_of(k), :], g_all.at[m, rows_of(k), :], x_s.at[k], x_r.at[k],
                        {"section": s - 1})

        @pl.when(s != last)
        def _():
            @pl.loop(0, PIECES)
            def _(k):
                c_tx[rows_of(k), :] = gather_sum(k).astype(BF16)
                to_last(k).start()

        wo_spread[1].relay()
        for spread in wo_spread:
            spread.finish()

        def g_copy(k, index, to, sem):
            slot = g_all.at[index, rows_of(k), :]
            return copy(slot, slot, g_s.at[sem, k], g_r.at[index, k], {"mp": to})

        def g_pushes():
            out = [(m, q * cores + core) for q in others(chip, chips)]
            out += [(m, chip * cores + e) for e in others(core, cores)]
            for q in sources(chip, chips):
                out += [(q * cores + core, chip * cores + e) for e in others(core, cores)]
            return out

        pushes = g_pushes()
        first_pushes = chips - 1 + cores - 1

        @pl.loop(0, PIECES)
        def _(k):
            at = tile(m * PIECES + k, piece)

            @pl.when(s == last)
            def _():
                total = gather_sum(k)
                for t in range(last):
                    copy(c_tx.at[rows_of(k), :], c_rx.at[t, rows_of(k), :], c_s.at[k], c_r.at[t, k],
                         {"section": t}).wait_recv()
                    total = total + c_rx[t, rows_of(k), :].astype(F32)
                unit, length = unit_rows(text[at, :])
                g_all[m, rows_of(k), :] = unit_backward(unit, length, mult * total).astype(BF16)

            @pl.when(s != last)
            def _():
                copy(g_new.at[rows_of(k), :], g_all.at[m, rows_of(k), :], x_s.at[k], x_r.at[k],
                     {"section": s + 1}).wait_recv()

            for i, (index, to) in enumerate(pushes[:first_pushes]):
                g_copy(k, index, to, i).start()

            g = g_all[m, rows_of(k), :]
            acc = g.astype(F32)
            for j in range(n_mp):
                grad = (dot_nt(g, wo_all[j]) * slope_own[j, rows_of(k), :]).astype(BF16)
                acc = acc + dot_nt(grad, wi_all[j])
            g_new[rows_of(k), :] = acc.astype(BF16)

            @pl.when(s > 0)
            def _():
                to_below(k).start()

        for k in range(PIECES):
            for q in sources(chip, chips):
                index = q * cores + core
                g_copy(k, index, lax.rem(m + 1, n_mp), 0).wait_recv()
            for i, (index, to) in enumerate(pushes[first_pushes:]):
                g_copy(k, index, to, first_pushes + i).start()

        def slab(k):
            return input_out.at[tile(k, quarter), :]

        def final(t):
            return copy(g_new.at[:, t * width : (t + 1) * width], slab(m), ix_s.at[t], ix_r,
                        {"section": t})

        @pl.when(s == 0)
        def _():
            for t in range(1, n_sec):
                final(t).start()
            input_out[mine, :] = g_new[:, 0:width]

        for k in range(PIECES):
            for e in sources(core, cores):
                for q in [chip] + sources(chip, chips):
                    index = q * cores + e
                    g_copy(k, index, lax.rem(m + 1, n_mp), 0).wait_recv()

        weight_sent = []

        def send_weights(which, grad):
            for p in range(n_dp):
                w_tx[p, which] = grad[p * share : (p + 1) * share, :].astype(BF16)
            for p in far:
                c = copy(w_tx.at[p, which], w_rx.at[d, which], w_s.at[which, p],
                         w_r.at[which, d], {"dp": p})
                c.start()
                weight_sent.append(c)

        send_weights(1, dot_tn(g_all[...].reshape(rows, feats), act_all[...]))

        @pl.loop(0, n_mp)
        def _(r):
            back = dot_nt(g_all[r], wo_all[m])
            pre_all[tile(r, quarter), :] = (back * slope_all[tile(r, quarter), :]).astype(BF16)

        send_weights(0, dot_tn(hidden[...], pre_all[...]))

        in_spread = Spread(slab, in_s, in_r)

        @pl.when(s != 0)
        def _():
            copy(g_new.at[:, 0:width], slab(m), ix_s.at[0], ix_r, {"section": 0}).wait_recv()

        in_spread.start()

        total = i_tx[d].astype(F32)
        for p in near:
            copy(i_tx.at[p], i_rx.at[p], im_s.at[p], im_r.at[p], {"dp": p}).wait_recv()
            total = total + i_rx[p].astype(F32)
        unit, length = unit_rows(image[mine_half, :])
        image_out[mine_half, :] = unit_backward(unit, length, mult * total).astype(BF16)
        out_sent = []
        for t in others(s, n_sec):
            c = copy(image_out.at[mine_half, :], image_out.at[mine_half, :],
                     io_s.at[t], io_r.at[s], {"section": t})
            c.start()
            out_sent.append(c)

        in_spread.relay()
        in_spread.finish()

        for t in sources(s, n_sec):
            part = image_out.at[tile(t, half), :]
            copy(part, part, io_s.at[t], io_r.at[t], {"section": t}).wait_recv()

        for c in gathers + col_sent + row_sent + a_sent + b_sent + image_sent + out_sent:
            c.wait_send()
        for spread in [wi_spread, in_spread] + wo_spread:
            spread.drain()
        for k in range(PIECES):
            for i, (index, to) in enumerate(pushes):
                g_copy(k, index, to, i).wait_send()

        @pl.when(s != last)
        def _():
            for k in range(PIECES):
                to_last(k).wait_send()

        @pl.when(s > 0)
        def _():
            for k in range(PIECES):
                to_below(k).wait_send()

        @pl.when(s == 0)
        def _():
            for t in range(1, n_sec):
                final(t).wait_send()

        for which, out in ((1, second_out), (0, first_out)):
            total = w_tx[d, which].astype(F32)
            for p in near:
                copy(w_tx.at[p, which], w_rx.at[p, which], w_s.at[which, p],
                     w_r.at[which, p], {"dp": p}).wait_recv()
                total = total + w_rx[p, which].astype(F32)
            out[...] = total
        for c in weight_sent:
            c.wait_send()

    return kernel


def store(image, inputs, first, second, image_out, input_out, first_out, second_out, sems):
    copies = [
        pltpu.make_async_copy(image, image_out, sems.at[0]),
        pltpu.make_async_copy(inputs, input_out, sems.at[1]),
        pltpu.make_async_copy(first, first_out.at[0], sems.at[2]),
        pltpu.make_async_copy(second, second_out.at[0], sems.at[3]),
    ]
    for c in copies:
        c.start()
    for c in copies:
        c.wait()


def solution(mesh):
    n_sec, n_dp, n_mp = mesh.shape["section"], mesh.shape["dp"], mesh.shape["mp"]

    def body(text, image, scale, hidden, w_in, w_out):
        rows, feats = text.shape
        own = image.shape[0]
        hid = w_in.shape[2]
        quarter, half, share = rows // n_mp, own // n_sec, feats // n_dp
        columns = half * n_dp
        cores = 2 if n_mp % 2 == 0 else 1
        chips = n_mp // cores
        dma = pltpu.SemaphoreType.DMA
        vmem = pl.BlockSpec(memory_space=pltpu.VMEM)
        hbm = pl.BlockSpec(memory_space=pl.ANY)
        out = pl.pallas_call(
            make_kernel(n_sec, n_dp, n_mp),
            out_shape=(
                jax.ShapeDtypeStruct((own, feats), BF16),
                jax.ShapeDtypeStruct((rows, feats // n_sec), BF16),
                jax.ShapeDtypeStruct((share, hid), F32),
                jax.ShapeDtypeStruct((share, hid), F32),
            ),
            in_specs=[hbm, hbm, pl.BlockSpec(memory_space=pltpu.SMEM), hbm, hbm, hbm],
            out_specs=(vmem,) * 4,
            scratch_shapes=[
                pltpu.VMEM((rows, feats), BF16),
                pltpu.VMEM((own, feats), BF16),
                pltpu.VMEM((rows, feats), BF16),
                pltpu.VMEM((rows, feats), BF16),
                pltpu.VMEM((columns, feats), BF16),
                pltpu.VMEM((rows, columns), F32),
                pltpu.VMEM((rows, columns), BF16),
                pltpu.VMEM((rows, LANES), F32),
                pltpu.VMEM((n_mp, quarter, LANES), F32),
                pltpu.VMEM((2 * n_mp, quarter), F32),
                pltpu.VMEM((n_sec * n_mp, 2 * n_mp, quarter), F32),
                pltpu.VMEM((2 * n_dp, half), F32),
                pltpu.VMEM((n_dp, 2 * n_dp, half), F32),
                pltpu.VMEM((n_mp, feats, hid), BF16),
                pltpu.VMEM((n_mp, hid, feats), BF16),
                pltpu.VMEM((n_mp, quarter, hid), F32),
                pltpu.VMEM((rows, hid), F32),
                pltpu.VMEM((rows, hid), BF16),
                pltpu.VMEM((rows, hid), BF16),
                pltpu.VMEM((chips, quarter, feats), BF16),
                pltpu.VMEM((chips, quarter, feats), BF16),
                pltpu.VMEM((chips, quarter, feats), BF16),
                pltpu.VMEM((chips, quarter, feats), BF16),
                pltpu.VMEM((quarter, feats), BF16),
                pltpu.VMEM((n_sec, quarter, feats), BF16),
                pltpu.VMEM((quarter, feats), F32),
                pltpu.VMEM((n_mp, quarter, feats), BF16),
                pltpu.VMEM((quarter, feats), BF16),
                pltpu.VMEM((n_dp, 2, share, hid), BF16),
                pltpu.VMEM((n_dp, 2, share, hid), BF16),
                pltpu.VMEM((n_dp, half, feats), BF16),
                pltpu.VMEM((n_dp, half, feats), BF16),
                dma((5,)),
                dma((n_dp,)), dma((n_dp,)),
                dma((n_dp,)), dma((n_dp,)),
                dma((n_sec * n_mp,)), dma((n_sec * n_mp,)),
                dma((2 * n_mp,)), dma((n_mp,)),
                dma((2, 2 * n_mp)), dma((2, n_mp)),
                dma((chips,)), dma((chips,)),
                dma((chips, PIECES)), dma((chips, PIECES)),
                dma((PIECES,)), dma((n_sec, PIECES)),
                dma((2 * n_mp, PIECES)), dma((n_mp, PIECES)),
                dma((PIECES,)), dma((PIECES,)),
                dma((2 * n_mp,)), dma((n_mp,)),
                dma((n_sec,)), dma,
                dma((2, n_dp)), dma((2, n_dp)),
                dma((n_dp,)), dma((n_dp,)),
                dma((n_sec,)), dma((n_sec,)),
            ],
            compiler_params=pltpu.CompilerParams(
                collective_id=0, has_side_effects=True, vmem_limit_bytes=63000000
            ),
        )(text, image, scale, hidden[0], w_in[0], w_out[0])
        return tuple(
            pl.pallas_call(
                store,
                out_shape=(
                    jax.ShapeDtypeStruct((own, feats), BF16),
                    jax.ShapeDtypeStruct((rows, feats // n_sec), BF16),
                    jax.ShapeDtypeStruct((1, share, hid), F32),
                    jax.ShapeDtypeStruct((1, share, hid), F32),
                ),
                in_specs=[vmem] * 4,
                out_specs=(hbm,) * 4,
                scratch_shapes=[dma((4,))],
                compiler_params=pltpu.CompilerParams(has_side_effects=True),
            )(*out)
        )

    return jax.shard_map(
        body,
        mesh=mesh,
        in_specs=(
            P("dp", None),
            P(("dp", "mp"), None),
            P(),
            P("section", "dp", None),
            P("section", None, "mp"),
            P("section", "mp", None),
        ),
        out_specs=(
            P(("dp", "mp"), None),
            P("dp", "section"),
            P("section", "dp", "mp"),
            P("section", "dp", "mp"),
        ),
        check_vma=False,
    )
```

time: 92.7 us -> 84.3 us (0.909)
  local copies, waits for them, and re-layouts: 4.57 us -> 0 us
  Pallas kernels: 86.6 us -> 82.2 us
    pallas_call x1, Pallas kernels: 86.6 us -> 79.9 us  [body(): pl.pallas_call(make_kernel(n_sec, n_dp, n_mp), out_shape=(jax.ShapeDtypeS...]
    unnamed x10 -> x0, local copies, waits for them, and re-layouts: 4.57 us -> none
    pallas_call x0 -> x1, Pallas kernels: none -> 2.35 us  [body(): pl.pallas_call(store, out_shape=(jax.ShapeDtypeStruct((own, feats), BF16)...]
where the time goes in v1:
time: 84.3 us; the launch traced here: 83.5 us
  Pallas kernels  82.2 us (98%)
  between operations  1.29 us (2%)
    pallas_call x1, Pallas kernels, body(): pl.pallas_call(make_kernel(n_sec, n_dp, n_mp), out_shape=(jax.ShapeDtypeS...  79.9 us
    pallas_call x1, Pallas kernels, body(): pl.pallas_call(store, out_shape=(jax.ShapeDtypeStruct((own, feats), BF16)...  2.35 us

profile of v1, /device:TPU:0, one launch (start us, length us, event | category | flops | bytes accessed | tf_op | source)
XLA Modules:
  0.0 83.5 jit_solution(8131552458118728041)
XLA Ops:
  1.3 79.9 %shard_map.93 = (bf16[256,512]{1,0:T(8,128)(2,1)}, bf16[1024,256]{1,0:T(8,128)(2,1)}, f32[128,512]{1,0:T(8,128)}, f32[128,512]{1,0:T(8,128)}) custom-call(bf16[1024,512]{1,0:T(8,128)(2,1)} %text_in.1, bf16[256,512]{1,0:T(8,128)(2,1)} %image_in.1, f32[1]{0:T(128)S(6)} %copy.10.scale_ref, bf16[1024,512]{1,0:T(8,128)(2,1)} %bitcast.3, ...), custom_call_target="tpu_custom_call" | custom-call | tf_op jit(solution)/shard_map/pallas_call | solution.py:572
  81.2 2.3 %shard_map.94 = (bf16[256,512]{1,0:T(8,128)(2,1)}, bf16[1024,256]{1,0:T(8,128)(2,1)}, f32[1,128,512]{2,1,0:T(8,128)}, f32[1,128,512]{2,1,0:T(8,128)}) custom-call(bf16[256,512]{1,0:T(8,128)(2,1)} %get-tuple-element.8.image, bf16[1024,256]{1,0:T(8,128)(2,1)} %get-tuple-element.9.inputs, f32[128,512]{1,0:T(8,128)} %get-tuple-element.10.first, ...), custom_call_target="tpu_custom_call" | custom-call | tf_op jit(solution)/shard_map/pallas_call | solution.py:637

commit v2 on v1

--- a/solution.py
+++ b/solution.py
@@ -59,12 +59,13 @@
         image_out, input_out, first_out, second_out,
         text, image, hidden,
         text_low, cols, scores, sgrad, row_max, row_lse, row_st, row_rx, col_st, col_rx,
-        wi_all, wo_all, slope_own, slope_all, act_all, pre_all,
+        raw_in, raw_out, wi_all, wo_all, slope_own, slope_all, act_all, pre_all,
         a_tx, a_rx, b_tx, b_rx, c_tx, c_rx, t_acc, g_all, g_new,
-        w_tx, w_rx, i_tx, i_rx,
-        ld, gat_s, gat_r, cs_s, cs_r, rs_s, rs_r, wi_s, wi_r, wo_s, wo_r,
+        w_tx, w_rx, w_via, i_tx, i_rx,
+        ld, gat_s, gat_r, cs_s, cs_r, rs_s, rs_r, wi_s, wi_r,
+        yo_s, yo_r, so_s, so_r, zo_s, zo_r, fo_s, fo_r,
         a_s, a_r, b_s, b_r, c_s, c_r, g_s, g_r, x_s, x_r, in_s, in_r, ix_s, ix_r,
-        w_s, w_r, im_s, im_r, io_s, io_r,
+        w_s, w_r, v_s, v_r, im_s, im_r, io_s, io_r,
     ):
         s = lax.axis_index("section")
         d = lax.axis_index("dp")
@@ -107,8 +108,8 @@
 
         loads = [
             pltpu.make_async_copy(image_in, image, ld.at[0]),
-            pltpu.make_async_copy(w_in, wi_all.at[m], ld.at[1]),
-            pltpu.make_async_copy(w_out, wo_all.at[m], ld.at[2]),
+            pltpu.make_async_copy(w_in, raw_in, ld.at[1]),
+            pltpu.make_async_copy(w_out, raw_out, ld.at[2]),
             pltpu.make_async_copy(text_in, text, ld.at[3]),
             pltpu.make_async_copy(hidden_in, hidden, ld.at[4]),
         ]
@@ -119,8 +120,6 @@
         loads[0].wait()
         own_unit, _ = unit_rows(image[mine_half, :])
         cols[tile(d, half), :] = own_unit.astype(BF16)
-        loads[1].wait()
-        loads[2].wait()
         pl.semaphore_wait(barrier, len(plane) + n_dp - 1)
 
         gathers = []
@@ -167,13 +166,65 @@
                 for c in self.sent:
                     c.wait_send()
 
-        def cut(ref, n, k):
-            size = ref.shape[1] // n
-            return lambda j: ref.at[j, k * size : (k + 1) * size, :]
-
-        wi_spread = Spread(cut(wi_all, 1, 0), wi_s, wi_r)
-        wo_spread = [Spread(cut(wo_all, 2, k), wo_s.at[k], wo_r.at[k]) for k in range(2)]
-        wi_spread.start()
+        pairs = 2 if n_dp % 2 == 0 else 1
+        side = lax.rem(d, pairs)
+        depth = feats // pairs
+
+        def wo_part(index, k):
+            return wo_all.at[index, tile(k, depth), :]
+
+        loads[2].wait()
+        wo_all[m] = raw_out[...].T
+        wo_sent = []
+
+        def wo_push(ref, send, recv, to):
+            c = copy(ref, ref, send, recv, to)
+            c.start()
+            wo_sent.append(c)
+
+        for q in others(chip, chips):
+            wo_push(wo_part(m, side), yo_s.at[q], yo_r.at[m], {"mp": q * cores + core})
+        for e in others(core, cores):
+            wo_push(wo_all.at[m], so_s.at[e], so_r.at[m], {"mp": chip * cores + e})
+
+        loads[1].wait()
+        wi_all[m] = raw_in[...].T
+
+        def wi_spread_of(k):
+            return Spread(lambda j: wi_all.at[j, pl.ds(k * (hid // 2), hid // 2), :], wi_s.at[k], wi_r.at[k])
+
+        wi_spread = [wi_spread_of(k) for k in range(2)]
+        wi_spread[0].start()
+
+        def wo_across():
+            for q in sources(chip, chips):
+                index = q * cores + core
+                copy(wo_part(index, side), wo_part(index, side), yo_s.at[q], yo_r.at[index],
+                     {"mp": index}).wait_recv()
+                if pairs == 2:
+                    wo_push(wo_part(index, side), zo_s.at[q], zo_r.at[index], {"dp": d + 1 - 2 * side})
+                for e in others(core, cores):
+                    wo_push(wo_part(index, side), fo_s.at[q, 0], fo_r.at[index, 0], {"mp": chip * cores + e})
+
+        def wo_along():
+            for q in sources(chip, chips):
+                index = q * cores + core
+                if pairs == 2:
+                    copy(wo_part(index, 1 - side), wo_part(index, 1 - side), zo_s.at[q], zo_r.at[index],
+                         {"dp": d + 1 - 2 * side}).wait_recv()
+                    for e in others(core, cores):
+                        wo_push(wo_part(index, 1 - side), fo_s.at[q, 1], fo_r.at[index, 1],
+                                {"mp": chip * cores + e})
+
+        def wo_finish():
+            for e in sources(core, cores):
+                index = chip * cores + e
+                copy(wo_all.at[index], wo_all.at[index], so_s.at[e], so_r.at[index], {"mp": index}).wait_recv()
+                for q in sources(chip, chips):
+                    index = q * cores + e
+                    for k in range(pairs):
+                        at = wo_part(index, side if k == 0 else 1 - side)
+                        copy(at, at, fo_s.at[q, k], fo_r.at[index, k], {"mp": chip * cores + e}).wait_recv()
 
         loads[3].wait()
 
@@ -213,7 +264,7 @@
 
         @pl.loop(0, n_mp)
         def _(r):
-            act, slope = gelu_terms(dot_nn(hidden[tile(r, quarter), :], wi_all[m]))
+            act, slope = gelu_terms(dot_nn(hidden[tile(r, quarter), :], raw_in[...]))
             act_all[tile(r, quarter), :] = act.astype(BF16)
             slope_all[tile(r, quarter), :] = slope
 
@@ -231,6 +282,8 @@
             c = copy(col_st, col_rx.at[d], cs_s.at[p], cs_r.at[d], {"dp": p})
             c.start()
             col_sent.append(c)
+
+        wo_across()
 
         for r in range(n_mp):
             part = pl.ds(r * quarter, quarter)
@@ -252,7 +305,8 @@
             c.start()
             row_sent.append(c)
 
-        wo_spread[0].start()
+        wi_spread[1].start()
+        wi_spread[0].relay()
 
         def merge(rx, count, n):
             peak = rx[0, 0:n, :]
@@ -329,7 +383,6 @@
                          {"mp": q * cores + core})
                 c.start()
                 b_sent.append(c)
-        wo_spread[1].start()
         for_sibling(chip)
         score_rows(m)
         score_diagonal()
@@ -347,16 +400,23 @@
         i_tx[d] = image_part(d).astype(BF16)
 
         from_sibling(chip)
-        wi_spread.relay()
-        wi_spread.finish()
         mine = tile(m, quarter)
-
-        @pl.loop(0, n_mp)
-        def _(j):
-            _, slope = gelu_terms(dot_nn(hidden[mine, :], wi_all[j]))
+        wi_spread[1].relay()
+        wo_along()
+
+        def own_slope(j):
+            _, slope = gelu_terms(dot_nt(hidden[mine, :], wi_all[j]))
             slope_own[j] = slope
 
-        wo_spread[0].relay()
+        own_slope(m)
+        for spread in wi_spread:
+            spread.finish()
+
+        @pl.loop(1, n_mp)
+        def _(k):
+            own_slope(lax.rem(m + k, n_mp))
+
+        wo_finish()
 
         def gather_sum(k):
             total = t_acc[rows_of(k), :]
@@ -381,9 +441,6 @@
                 c_tx[rows_of(k), :] = gather_sum(k).astype(BF16)
                 to_last(k).start()
 
-        wo_spread[1].relay()
-        for spread in wo_spread:
-            spread.finish()
 
         def g_copy(k, index, to, sem):
             slot = g_all.at[index, rows_of(k), :]
@@ -424,8 +481,8 @@
             g = g_all[m, rows_of(k), :]
             acc = g.astype(F32)
             for j in range(n_mp):
-                grad = (dot_nt(g, wo_all[j]) * slope_own[j, rows_of(k), :]).astype(BF16)
-                acc = acc + dot_nt(grad, wi_all[j])
+                grad = (dot_nn(g, wo_all[j]) * slope_own[j, rows_of(k), :]).astype(BF16)
+                acc = acc + dot_nn(grad, wi_all[j])
             g_new[rows_of(k), :] = acc.astype(BF16)
 
             @pl.when(s > 0)
@@ -459,25 +516,47 @@
                     g_copy(k, index, lax.rem(m + 1, n_mp), 0).wait_recv()
 
         weight_sent = []
+        via_hub = n_dp == 4
+        end = (d == 0) | (d == n_dp - 1)
+        hub = jnp.where(d == 0, 1, n_dp - 2)
+
+        def to_dp(which, p):
+            return copy(w_tx.at[p, which], w_rx.at[d, which], w_s.at[which, p], w_r.at[which, d], {"dp": p})
+
+        def to_hub(which):
+            return copy(w_tx.at[far[0], which], w_via.at[which], v_s.at[which], v_r.at[which], {"dp": hub})
 
         def send_weights(which, grad):
             for p in range(n_dp):
                 w_tx[p, which] = grad[p * share : (p + 1) * share, :].astype(BF16)
-            for p in far:
-                c = copy(w_tx.at[p, which], w_rx.at[d, which], w_s.at[which, p],
-                         w_r.at[which, d], {"dp": p})
+            if via_hub:
+                @pl.when(end)
+                def _():
+                    to_hub(which).start()
+            for p in far[1:] if via_hub else far:
+                c = to_dp(which, p)
                 c.start()
                 weight_sent.append(c)
 
+        def pass_on(which):
+            if via_hub:
+                @pl.when(jnp.logical_not(end))
+                def _():
+                    to_hub(which).wait_recv()
+                    both = w_tx[far[0], which].astype(F32) + w_via[which].astype(F32)
+                    w_tx[far[0], which] = both.astype(BF16)
+                    to_dp(which, far[0]).start()
+
         send_weights(1, dot_tn(g_all[...].reshape(rows, feats), act_all[...]))
 
         @pl.loop(0, n_mp)
         def _(r):
-            back = dot_nt(g_all[r], wo_all[m])
+            back = dot_nn(g_all[r], wo_all[m])
             pre_all[tile(r, quarter), :] = (back * slope_all[tile(r, quarter), :]).astype(BF16)
 
         send_weights(0, dot_tn(hidden[...], pre_all[...]))
 
+        pass_on(1)
         in_spread = Spread(slab, in_s, in_r)
 
         @pl.when(s != 0)
@@ -500,6 +579,7 @@
             out_sent.append(c)
 
         in_spread.relay()
+        pass_on(0)
         in_spread.finish()
 
         for t in sources(s, n_sec):
@@ -508,8 +588,10 @@
 
         for c in gathers + col_sent + row_sent + a_sent + b_sent + image_sent + out_sent:
             c.wait_send()
-        for spread in [wi_spread, in_spread] + wo_spread:
+        for spread in wi_spread + [in_spread]:
             spread.drain()
+        for c in wo_sent:
+            c.wait_send()
         for k in range(PIECES):
             for i, (index, to) in enumerate(pushes):
                 g_copy(k, index, to, i).wait_send()
@@ -530,14 +612,29 @@
                 final(t).wait_send()
 
         for which, out in ((1, second_out), (0, first_out)):
-            total = w_tx[d, which].astype(F32)
-            for p in near:
-                copy(w_tx.at[p, which], w_rx.at[p, which], w_s.at[which, p],
-                     w_r.at[which, p], {"dp": p}).wait_recv()
-                total = total + w_rx[p, which].astype(F32)
-            out[...] = total
+            out[...] = w_tx[d, which].astype(F32)
+
+            def add(p):
+                copy(w_tx.at[p, which], w_rx.at[p, which], w_s.at[which, p], w_r.at[which, p],
+                     {"dp": p}).wait_recv()
+                out[...] += w_rx[p, which].astype(F32)
+
+            for k, p in enumerate(near):
+                if via_hub and k == n_dp - 2:
+                    pl.when(jnp.logical_not(end))(lambda p=p: add(p))
+                else:
+                    add(p)
         for c in weight_sent:
             c.wait_send()
+        if via_hub:
+            for which in range(2):
+                @pl.when(end)
+                def _():
+                    to_hub(which).wait_send()
+
+                @pl.when(jnp.logical_not(end))
+                def _():
+                    to_dp(which, far[0]).wait_send()
 
     return kernel
 
@@ -568,14 +665,14 @@
         chips = n_mp // cores
         dma = pltpu.SemaphoreType.DMA
         vmem = pl.BlockSpec(memory_space=pltpu.VMEM)
-        hbm = pl.BlockSpec(memory_space=pl.ANY)
+        hbm = pl.BlockSpec(memory_space=pltpu.HBM)
         out = pl.pallas_call(
             make_kernel(n_sec, n_dp, n_mp),
             out_shape=(
-                jax.ShapeDtypeStruct((own, feats), BF16),
-                jax.ShapeDtypeStruct((rows, feats // n_sec), BF16),
-                jax.ShapeDtypeStruct((share, hid), F32),
-                jax.ShapeDtypeStruct((share, hid), F32),
+                pltpu.VMEM((own, feats), BF16),
+                pltpu.VMEM((rows, feats // n_sec), BF16),
+                pltpu.VMEM((share, hid), F32),
+                pltpu.VMEM((share, hid), F32),
             ),
             in_specs=[hbm, hbm, pl.BlockSpec(memory_space=pltpu.SMEM), hbm, hbm, hbm],
             out_specs=(vmem,) * 4,
@@ -593,8 +690,10 @@
                 pltpu.VMEM((n_sec * n_mp, 2 * n_mp, quarter), F32),
                 pltpu.VMEM((2 * n_dp, half), F32),
                 pltpu.VMEM((n_dp, 2 * n_dp, half), F32),
+                pltpu.VMEM((feats, hid), BF16),
+                pltpu.VMEM((hid, feats), BF16),
+                pltpu.VMEM((n_mp, hid, feats), BF16),
                 pltpu.VMEM((n_mp, feats, hid), BF16),
-                pltpu.VMEM((n_mp, hid, feats), BF16),
                 pltpu.VMEM((n_mp, quarter, hid), F32),
                 pltpu.VMEM((rows, hid), F32),
                 pltpu.VMEM((rows, hid), BF16),
@@ -610,14 +709,16 @@
                 pltpu.VMEM((quarter, feats), BF16),
                 pltpu.VMEM((n_dp, 2, share, hid), BF16),
                 pltpu.VMEM((n_dp, 2, share, hid), BF16),
+                pltpu.VMEM((2, share, hid), BF16),
                 pltpu.VMEM((n_dp, half, feats), BF16),
                 pltpu.VMEM((n_dp, half, feats), BF16),
                 dma((5,)),
                 dma((n_dp,)), dma((n_dp,)),
                 dma((n_dp,)), dma((n_dp,)),
                 dma((n_sec * n_mp,)), dma((n_sec * n_mp,)),
-                dma((2 * n_mp,)), dma((n_mp,)),
                 dma((2, 2 * n_mp)), dma((2, n_mp)),
+                dma((chips,)), dma((n_mp,)), dma((cores,)), dma((n_mp,)),
+                dma((chips,)), dma((n_mp,)), dma((chips, 2)), dma((n_mp, 2)),
                 dma((chips,)), dma((chips,)),
                 dma((chips, PIECES)), dma((chips, PIECES)),
                 dma((PIECES,)), dma((n_sec, PIECES)),
@@ -626,13 +727,15 @@
                 dma((2 * n_mp,)), dma((n_mp,)),
                 dma((n_sec,)), dma,
                 dma((2, n_dp)), dma((2, n_dp)),
+                dma((2,)), dma((2,)),
                 dma((n_dp,)), dma((n_dp,)),
                 dma((n_sec,)), dma((n_sec,)),
             ],
             compiler_params=pltpu.CompilerParams(
-                collective_id=0, has_side_effects=True, vmem_limit_bytes=63000000
+                collective_id=0, has_side_effects=True, vmem_limit_bytes=50000000
             ),
-        )(text, image, scale, hidden[0], w_in[0], w_out[0])
+        )(*(pltpu.with_memory_space_constraint(x, pltpu.HBM) for x in (text, image)), scale,
+          *(pltpu.with_memory_space_constraint(x[0], pltpu.HBM) for x in (hidden, w_in, w_out)))
         return tuple(
             pl.pallas_call(
                 store,
@@ -646,7 +749,7 @@
                 out_specs=(hbm,) * 4,
                 scratch_shapes=[dma((4,))],
                 compiler_params=pltpu.CompilerParams(has_side_effects=True),
-            )(*out)
+            )(*(pltpu.with_memory_space_constraint(x, pltpu.VMEM) for x in out))
         )
 
     return jax.shard_map(

time: 84.3 us -> 71.5 us (0.85)
  Pallas kernels: 82.2 us -> 70.1 us
    pallas_call x1, Pallas kernels: 79.9 us -> 69 us  [body(): pl.pallas_call(make_kernel(n_sec, n_dp, n_mp), out_shape=(pltpu.VMEM((own...]
    pallas_call x1, Pallas kernels: 2.35 us -> 1.09 us  [body(): pl.pallas_call(store, out_shape=(jax.ShapeDtypeStruct((own, feats), BF16)...]
where the time goes in v2:
time: 71.5 us; the launch traced here: 71.4 us
  Pallas kernels  70.1 us (98%)
  between operations  1.29 us (2%)
    pallas_call x1, Pallas kernels, body(): pl.pallas_call(make_kernel(n_sec, n_dp, n_mp), out_shape=(pltpu.VMEM((own...  69 us

profile of v2, /device:TPU:0, one launch (start us, length us, event | category | flops | bytes accessed | tf_op | source)
XLA Modules:
  0.0 71.4 jit_solution(15794675410387113208)
XLA Ops:
  1.3 69.0 %shard_map.93 = (bf16[256,512]{1,0:T(8,128)(2,1)S(1)}, bf16[1024,256]{1,0:T(8,128)(2,1)S(1)}, f32[128,512]{1,0:T(8,128)S(1)}, f32[128,512]{1,0:T(8,128)S(1)}) custom-call(bf16[1024,512]{1,0:T(8,128)(2,1)} %text_in.1, bf16[256,512]{1,0:T(8,128)(2,1)} %image_in.1, f32[1]{0:T(128)S(6)} %copy.10.scale_ref, bf16[1024,512]{1,0:T(8,128)(2,1)} %bitcast.3, ...), custom_call_target="tpu_custom_call" | custom-call | tf_op jit(solution)/shard_map/pallas_call | solution.py:669
  70.3 1.1 %shard_map.94 = (bf16[256,512]{1,0:T(8,128)(2,1)}, bf16[1024,256]{1,0:T(8,128)(2,1)}, f32[1,128,512]{2,1,0:T(8,128)}, f32[1,128,512]{2,1,0:T(8,128)}) custom-call(bf16[256,512]{1,0:T(8,128)(2,1)S(1)} %get-tuple-element.8.image, bf16[1024,256]{1,0:T(8,128)(2,1)S(1)} %get-tuple-element.9.inputs, f32[128,512]{1,0:T(8,128)S(1)} %get-tuple-element.10.first, ...), custom_call_target="tpu_custom_call" | custom-call | tf_op jit(solution)/shard_map/pallas_call | solution.py:740

commit v3 on v2

v3 whole, which is shorter than its diff:
```python
import jax
import jax.numpy as jnp
from jax import lax
from jax.experimental import pallas as pl
from jax.experimental.pallas import tpu as pltpu
from jax.sharding import PartitionSpec as P

MESH = pl.DeviceIdType.MESH
F32 = jnp.float32
BF16 = jnp.bfloat16
GELU = 1.702
LANES = 128
PIECES = 8
GROUP = 2


def unit_rows(values):
    wide = values.astype(F32)
    length = jnp.sqrt(jnp.sum(wide * wide, axis=1, keepdims=True) + 1.0)
    return (wide / length, length)


def unit_backward(unit, length, grad_unit):
    return (grad_unit - unit * jnp.sum(unit * grad_unit, axis=1, keepdims=True)) / length


def dot_nn(a, b):
    return lax.dot_general(a, b, (((1,), (0,)), ((), ())), preferred_element_type=F32)


def dot_nt(a, b):
    return lax.dot_general(a, b, (((1,), (1,)), ((), ())), preferred_element_type=F32)


def dot_tn(a, b):
    return lax.dot_general(a, b, (((0,), (0,)), ((), ())), preferred_element_type=F32)


def tile(index, size):
    return pl.ds(pl.multiple_of(index * size, size), size)


def pick(index, values):
    out = 0
    for k, v in enumerate(values):
        out = out + jnp.where(index == k, v, 0)
    return out


def nearest(count):
    return [sorted((p for p in range(count) if p != i), key=lambda p: (abs(p - i), p)) for i in range(count)]


def make_kernel(n_sec, n_dp, n_mp):
    cores = 2 if n_mp % 2 == 0 else 1
    chips = n_mp // cores

    def kernel(
        text_in, image_in, scale_ref, hidden_in, w_in, w_out,
        image_out, input_out, first_out, second_out,
        text, image, hidden,
        text_low, cols, scores, sgrad, row_max, row_sum, row_lse, row_st, row_rx, col_st, col_rx,
        raw_in, raw_out, wi_all, wo_all, slope_own, slope_all, act_all, pre_all, grad_own,
        a_tx, a_rx, b_tx, b_rx, c_tx, c_rx, t_acc, g_all, g_new,
        w_tx, w_rx, w_via, i_tx, i_rx,
        ld, gat_s, gat_r, cs_s, cs_r, rs_s, rs_r, wi_s, wi_a, wi_i,
        wo_s, yo_r, so_r, zo_r, fo_r, a_s, a_r, b_s, b_r, c_s, c_r, g_s, ga_r, gi_r, x_s, x_r,
        in_s, in_a, in_i, ix_s, ix_r, w_s, w_r, v_r, im_s, im_r, io_s, io_r,
    ):
        s = lax.axis_index("section")
        d = lax.axis_index("dp")
        m = lax.axis_index("mp")
        last = n_sec - 1
        rows, feats = text.shape
        own = image.shape[0]
        half = own // n_sec
        quarter = rows // n_mp
        piece = quarter // PIECES
        hid = slope_all.shape[1]
        share = feats // n_dp
        width = feats // n_sec
        mult = scale_ref[0]
        core = lax.rem(m, cores)
        chip = m // cores

        def copy(src, dst, send, recv, where):
            return pltpu.make_async_remote_copy(
                src_ref=src, dst_ref=dst, send_sem=send, recv_sem=recv,
                device_id=where, device_id_type=MESH,
            )

        def wait_sent(ref, sem):
            pltpu.make_async_copy(ref, ref, sem).wait()

        def others(mine, count):
            return [lax.rem(mine + k, count) for k in range(1, count)]

        def sources(mine, count):
            return [lax.rem(mine + count - k, count) for k in range(1, count)]

        order = nearest(n_dp)
        near = [pick(d, [order[i][k] for i in range(n_dp)]) for k in range(n_dp - 1)]
        far = near[::-1]

        barrier = pltpu.get_barrier_semaphore()
        plane = [(t, p) for t in [s] + others(s, n_sec) for p in [m] + others(m, n_mp)][1:]
        for t, p in plane:
            pl.semaphore_signal(barrier, inc=1, device_id={"section": t, "mp": p}, device_id_type=MESH)
        for p in near:
            pl.semaphore_signal(barrier, inc=1, device_id={"dp": p}, device_id_type=MESH)

        loads = [
            pltpu.make_async_copy(image_in, image, ld.at[0]),
            pltpu.make_async_copy(w_in, raw_in, ld.at[1]),
            pltpu.make_async_copy(w_out, raw_out, ld.at[2]),
            pltpu.make_async_copy(text_in, text, ld.at[3]),
            pltpu.make_async_copy(hidden_in, hidden, ld.at[4]),
        ]
        for c in loads:
            c.start()

        mine_half = tile(s, half)
        loads[0].wait()
        own_unit, _ = unit_rows(image[mine_half, :])
        cols[tile(d, half), :] = own_unit.astype(BF16)
        pl.semaphore_wait(barrier, len(plane) + n_dp - 1)

        for p in far:
            copy(cols.at[tile(d, half), :], cols.at[tile(d, half), :], gat_s, gat_r.at[d], {"dp": p}).start()

        class Spread:
            def __init__(self, slot, send, across, inside):
                self.slot, self.send, self.across, self.inside = slot, send, across, inside

            def push(self, index, recv, to):
                copy(self.slot(index), self.slot(index), self.send, recv, {"mp": to}).start()

            def start(self):
                for q in others(chip, chips):
                    self.push(m, self.across.at[chip], q * cores + core)
                for e in others(core, cores):
                    self.push(m, self.inside.at[chip], chip * cores + e)

            def relay(self):
                for q in sources(chip, chips):
                    index = q * cores + core
                    copy(self.slot(index), self.slot(index), self.send, self.across.at[q], {"mp": index}).wait_recv()
                    for e in others(core, cores):
                        self.push(index, self.inside.at[q], chip * cores + e)

            def finish(self):
                for e in sources(core, cores):
                    for q in range(chips):
                        slot = self.slot(q * cores + e)
                        copy(slot, slot, self.send, self.inside.at[q], {"mp": chip * cores + e}).wait_recv()

        pairs = 2 if n_dp % 2 == 0 else 1
        side = lax.rem(d, pairs)
        depth = feats // pairs

        def wo_part(index, k):
            return wo_all.at[index, tile(k, depth), :]

        loads[2].wait()
        wo_all[m] = raw_out[...].T
        def wo_push(ref, recv, to):
            copy(ref, ref, wo_s, recv, to).start()

        for q in others(chip, chips):
            wo_push(wo_part(m, side), yo_r.at[chip], {"mp": q * cores + core})
        for e in others(core, cores):
            wo_push(wo_all.at[m], so_r, {"mp": chip * cores + e})

        loads[1].wait()
        wi_all[m] = raw_in[...].T

        def wi_spread_of(k):
            return Spread(lambda j: wi_all.at[j, pl.ds(k * (hid // 2), hid // 2), :], wi_s, wi_a.at[k], wi_i.at[k])

        wi_spread = [wi_spread_of(k) for k in range(2)]
        wi_spread[0].start()

        def wo_across():
            for q in sources(chip, chips):
                index = q * cores + core
                at = wo_part(index, side)
                copy(at, at, wo_s, yo_r.at[q], {"mp": index}).wait_recv()
                if pairs == 2:
                    wo_push(at, zo_r.at[q], {"dp": d + 1 - 2 * side})
                for e in others(core, cores):
                    wo_push(at, fo_r.at[q, 0], {"mp": chip * cores + e})

        def wo_along():
            for q in sources(chip, chips):
                at = wo_part(q * cores + core, 1 - side)
                if pairs == 2:
                    copy(at, at, wo_s, zo_r.at[q], {"dp": d + 1 - 2 * side}).wait_recv()
                    for e in others(core, cores):
                        wo_push(at, fo_r.at[q, 1], {"mp": chip * cores + e})

        def wo_finish():
            for e in sources(core, cores):
                to = {"mp": chip * cores + e}
                own_block = wo_all.at[chip * cores + e]
                copy(own_block, own_block, wo_s, so_r, to).wait_recv()
                for q in sources(chip, chips):
                    for k in range(pairs):
                        at = wo_part(q * cores + e, side if k == 0 else 1 - side)
                        copy(at, at, wo_s, fo_r.at[q, k], to).wait_recv()

        loads[3].wait()

        @pl.loop(0, n_mp)
        def _(r):
            unit, _ = unit_rows(text[tile(r, quarter), :])
            text_low[tile(r, quarter), :] = unit.astype(BF16)

        row_max[...] = jnp.full(row_max.shape, -1e30, F32)
        row_sum[...] = jnp.zeros(row_sum.shape, F32)

        def block_scores(p):
            block = cols[tile(p, half), :]
            peak = jnp.full((1, half), -1e30, F32)
            for r in range(n_mp):
                part = pl.ds(r * quarter, quarter)
                value = mult * dot_nt(text_low[part, :], block)
                scores[part, tile(p, half)] = value
                peak = jnp.maximum(peak, jnp.max(value, axis=0, keepdims=True))
            acc = jnp.zeros((1, half), F32)
            for r in range(n_mp):
                value = scores[pl.ds(r * quarter, quarter), tile(p, half)]
                acc = acc + jnp.sum(jnp.exp(value - peak), axis=0, keepdims=True)
            col_st[pl.ds(p, 1), :] = peak
            col_st[pl.ds(n_dp + p, 1), :] = acc

        def block_rows(p):
            for r in range(n_mp):
                part = pl.ds(r * quarter, quarter)
                old = row_max[part, :]
                best = old
                value = [scores[part, pl.ds(pl.multiple_of(p * half + k, LANES), LANES)] for k in range(0, half, LANES)]
                for v in value:
                    best = jnp.maximum(best, v)
                acc = row_sum[part, :] * jnp.exp(old - best)
                for v in value:
                    acc = acc + jnp.exp(v - best)
                row_max[part, :] = best
                row_sum[part, :] = acc

        block_scores(d)
        block_rows(d)

        def gelu_terms(pre):
            sigm = 1.0 / (1.0 + jnp.exp(-GELU * pre))
            return pre * sigm, sigm + GELU * pre * sigm * (1.0 - sigm)

        loads[4].wait()

        @pl.loop(0, n_mp)
        def _(r):
            act, slope = gelu_terms(dot_nn(hidden[tile(r, quarter), :], raw_in[...]))
            act_all[tile(r, quarter), :] = act.astype(BF16)
            slope_all[tile(r, quarter), :] = slope

        @pl.loop(0, n_dp - 1)
        def _(k):
            p = near[0]
            for i in range(1, n_dp - 1):
                p = jnp.where(k == i, near[i], p)
            copy(cols.at[tile(p, half), :], cols.at[tile(p, half), :], gat_s, gat_r.at[p], {"dp": p}).wait_recv()
            block_scores(p)

            @pl.when(k < n_dp - 2)
            def _():
                block_rows(p)

        col_rx[d] = col_st[...]
        for p in far:
            copy(col_st, col_rx.at[d], cs_s, cs_r.at[d], {"dp": p}).start()

        wo_across()
        block_rows(far[0])

        for r in range(n_mp):
            part = pl.ds(r * quarter, quarter)
            peak = jnp.max(row_max[part, :], axis=1, keepdims=True)
            acc = jnp.sum(row_sum[part, :] * jnp.exp(row_max[part, :] - peak), axis=1, keepdims=True)
            wide_peak = jnp.broadcast_to(peak, (quarter, LANES)).T
            wide_sum = jnp.broadcast_to(acc, (quarter, LANES)).T
            row_st[r : r + 1, :] = wide_peak[0:1, :]
            row_st[n_mp + r : n_mp + r + 1, :] = wide_sum[0:1, :]

        here = s * n_mp + m
        row_rx[here] = row_st[...]
        for k, (t, p) in enumerate(plane):
            copy(row_st, row_rx.at[here], rs_s, rs_r.at[here], {"section": t, "mp": p}).start()

        wi_spread[1].start()
        wi_spread[0].relay()

        def merge(rx, count, n):
            peak = rx[0, 0:n, :]
            for k in range(1, count):
                peak = jnp.maximum(peak, rx[k, 0:n, :])
            acc = jnp.zeros(peak.shape, F32)
            for k in range(count):
                acc = acc + rx[k, n : 2 * n, :] * jnp.exp(rx[k, 0:n, :] - peak)
            return peak + jnp.log(acc)

        for p in near:
            copy(col_st, col_rx.at[p], cs_s, cs_r.at[p], {"dp": p}).wait_recv()
        col_lse = merge(col_rx, n_dp, n_dp)
        for t, p in plane:
            copy(row_st, row_rx.at[t * n_mp + p], rs_s, rs_r.at[t * n_mp + p], {"section": t, "mp": p}).wait_recv()
        merged = merge(row_rx, n_sec * n_mp, n_mp)
        for r in range(n_mp):
            row_lse[r] = jnp.broadcast_to(merged[r : r + 1, :], (LANES, quarter)).T

        def score_rows(r):
            line = row_lse[r]
            for p in range(n_dp):
                for k in range(0, half, LANES):
                    at = pl.ds(p * half + k, LANES)
                    value = scores[tile(r, quarter), at]
                    both = jnp.exp(value - line) + jnp.exp(value - col_lse[p : p + 1, k : k + LANES])
                    sgrad[tile(r, quarter), at] = (0.5 * both).astype(BF16)

        def score_diagonal():
            line = row_lse[m]
            text_id = lax.broadcasted_iota(jnp.int32, (quarter, LANES), 0)
            lse = col_lse[0:1, :]
            for p in range(1, n_dp):
                lse = jnp.where(d == p, col_lse[p : p + 1, :], lse)
            for k in range(0, half, LANES):
                at = pl.ds(pl.multiple_of(d * half + k, LANES), LANES)
                value = scores[tile(m, quarter), at]
                both = jnp.exp(value - line) + jnp.exp(value - lse[:, k : k + LANES])
                image_id = lax.broadcasted_iota(jnp.int32, (quarter, LANES), 1) + (s * half + k)
                out = 0.5 * both - jnp.where(text_id == image_id, 1.0, 0.0)
                sgrad[tile(m, quarter), at] = out.astype(BF16)

        def text_part(r):
            return dot_nn(sgrad[tile(r, quarter), :], cols[...])

        def rows_of(k):
            return tile(k, piece)

        def for_sibling(q):
            for e in others(core, cores):
                r = q * cores + e
                score_rows(r)
                a_tx[q] = text_part(r).astype(BF16)
                copy(a_tx.at[q], a_rx.at[q], a_s, a_r.at[q], {"mp": chip * cores + e}).start()

        def from_sibling(q):
            for e in others(core, cores):
                copy(a_tx.at[q], a_rx.at[q], a_s, a_r.at[q], {"mp": chip * cores + e}).wait_recv()
                t_acc[...] += a_rx[q].astype(F32)

        for q in others(chip, chips):
            for_sibling(q)
            score_rows(q * cores + core)
            t_acc[...] = text_part(q * cores + core)
            from_sibling(q)
            b_tx[q] = t_acc[...].astype(BF16)
            for k in range(PIECES):
                copy(b_tx.at[q, rows_of(k), :], b_rx.at[chip, rows_of(k), :], b_s, b_r.at[chip, k],
                     {"mp": q * cores + core}).start()
        for_sibling(chip)
        score_rows(m)
        score_diagonal()
        t_acc[...] = text_part(m)

        def image_part(p):
            return dot_tn(sgrad[:, tile(p, half)], text_low[...])

        for p in far:
            i_tx[p] = image_part(p).astype(BF16)
            copy(i_tx.at[p], i_rx.at[d], im_s, im_r.at[d], {"dp": p}).start()
        i_tx[d] = image_part(d).astype(BF16)

        from_sibling(chip)
        mine = tile(m, quarter)
        wi_spread[1].relay()
        wo_along()

        def gather_sum(k):
            total = t_acc[rows_of(k), :]
            for q in sources(chip, chips):
                copy(b_tx.at[q, rows_of(k), :], b_rx.at[q, rows_of(k), :], b_s, b_r.at[q, k],
                     {"mp": q * cores + core}).wait_recv()
                total = total + b_rx[q, rows_of(k), :].astype(F32)
            return total

        def to_last(k):
            return copy(c_tx.at[rows_of(k), :], c_rx.at[s, rows_of(k), :], c_s, c_r.at[s, k],
                        {"section": last})

        def to_below(k):
            return copy(g_new.at[rows_of(k), :], g_all.at[m, rows_of(k), :], x_s, x_r.at[k],
                        {"section": s - 1})

        @pl.when(s != last)
        def _():
            @pl.loop(0, PIECES)
            def _(k):
                c_tx[rows_of(k), :] = gather_sum(k).astype(BF16)
                to_last(k).start()

        def own_slope(j):
            _, slope = gelu_terms(dot_nt(hidden[mine, :], wi_all[j]))
            slope_own[j] = slope

        own_slope(m)
        for spread in wi_spread:
            spread.finish()

        @pl.loop(1, n_mp)
        def _(k):
            own_slope(lax.rem(m + k, n_mp))

        wo_finish()

        def g_push(k, index, recv, to):
            slot = g_all.at[index, rows_of(k), :]
            copy(slot, slot, g_s, recv, {"mp": to}).start()

        @pl.loop(0, PIECES // GROUP)
        def _(i):
            @pl.loop(i * GROUP, (i + 1) * GROUP)
            def _(k):
                at = tile(m * PIECES + k, piece)

                @pl.when(s == last)
                def _():
                    total = gather_sum(k)
                    for t in range(last):
                        copy(c_tx.at[rows_of(k), :], c_rx.at[t, rows_of(k), :], c_s, c_r.at[t, k],
                             {"section": t}).wait_recv()
                        total = total + c_rx[t, rows_of(k), :].astype(F32)
                    unit, length = unit_rows(text[at, :])
                    g_all[m, rows_of(k), :] = unit_backward(unit, length, mult * total).astype(BF16)

                @pl.when(s != last)
                def _():
                    copy(g_new.at[rows_of(k), :], g_all.at[m, rows_of(k), :], x_s, x_r.at[k],
                         {"section": s + 1}).wait_recv()

                for q in others(chip, chips):
                    g_push(k, m, ga_r.at[chip, k], q * cores + core)

            group = tile(i, GROUP * piece)
            for e in others(core, cores):
                slot = g_all.at[m, group, :]
                copy(slot, slot, g_s, gi_r.at[chip, i], {"mp": chip * cores + e}).start()
            g = g_all[m, group, :]
            for j in range(n_mp):
                back = dot_nn(g, wo_all[j])
                grad_own[:, j * hid : (j + 1) * hid] = (back * slope_own[j, group, :]).astype(BF16)
            acc = dot_nn(grad_own[...], wi_all[...].reshape(n_mp * hid, feats))
            g_new[group, :] = (g.astype(F32) + acc).astype(BF16)

            @pl.when(s > 0)
            def _():
                for k in range(GROUP):
                    to_below(i * GROUP + k).start()

        for i in range(PIECES // GROUP):
            group = pl.ds(i * GROUP * piece, GROUP * piece)
            for q in sources(chip, chips):
                index = q * cores + core
                for k in range(i * GROUP, (i + 1) * GROUP):
                    slot = g_all.at[index, rows_of(k), :]
                    copy(slot, slot, g_s, ga_r.at[q, k], {"mp": index}).wait_recv()
                slot = g_all.at[index, group, :]
                for e in others(core, cores):
                    copy(slot, slot, g_s, gi_r.at[q, i], {"mp": chip * cores + e}).start()

        def slab(k):
            return input_out.at[tile(k, quarter), :]

        def final(t):
            return copy(g_new.at[:, t * width : (t + 1) * width], slab(m), ix_s, ix_r,
                        {"section": t})

        @pl.when(s == 0)
        def _():
            for t in range(1, n_sec):
                final(t).start()
            input_out[mine, :] = g_new[:, 0:width]

        for i in range(PIECES // GROUP):
            for e in sources(core, cores):
                for q in range(chips):
                    slot = g_all.at[q * cores + e, pl.ds(i * GROUP * piece, GROUP * piece), :]
                    copy(slot, slot, g_s, gi_r.at[q, i], {"mp": chip * cores + e}).wait_recv()

        via_hub = n_dp == 4
        mate = d + 1 - 2 * lax.rem(d, 2)
        low = d < n_dp // 2
        end = (d == 0) | (d == n_dp - 1)
        inner = jnp.logical_not(end)
        cross = [jnp.where(low, n_dp - 1, 0), jnp.where(low, n_dp - 2, 1)]

        def weight_grad(which, at):
            if which == 1:
                left = g_all[:, :, at]
                return dot_tn(left.reshape(rows, left.shape[2]), act_all[...]).astype(BF16)
            return dot_tn(hidden[:, at], pre_all[...]).astype(BF16)

        def to_dp(which, p, slot):
            return copy(w_tx.at[p, which], w_rx.at[slot, which], w_s, w_r.at[which, slot], {"dp": p})

        def to_hub(which, k):
            return copy(w_tx.at[cross[k], which], w_via.at[which, k], w_s, v_r.at[which, k], {"dp": mate})

        def send_weights(which):
            if via_hub:
                for k in range(2):
                    w_tx[cross[k], which] = weight_grad(which, tile(cross[k], share))

                    @pl.when(end)
                    def _():
                        to_hub(which, k).start()

                w_tx[mate, which] = weight_grad(which, tile(mate, share))

                @pl.when(inner)
                def _():
                    to_dp(which, mate, 0).start()

                if which == 0:

                    @pl.when(end)
                    def _():
                        to_dp(1, mate, 0).start()
                        to_dp(0, mate, 0).start()

                w_tx[d, which] = weight_grad(which, tile(d, share))
            else:
                grad = weight_grad(which, pl.ds(0, feats))
                for p in range(n_dp):
                    w_tx[p, which] = grad[p * share : (p + 1) * share, :]
                for p in far:
                    to_dp(which, p, d).start()

        def pass_on(which, k):
            if via_hub:

                @pl.when(inner)
                def _():
                    to_hub(which, k).wait_recv()
                    both = w_tx[cross[k], which].astype(F32) + w_via[which, k].astype(F32)
                    w_tx[cross[k], which] = both.astype(BF16)
                    to_dp(which, cross[k], 1).start()

        send_weights(1)

        @pl.loop(0, n_mp)
        def _(r):
            back = dot_nn(g_all[r], wo_all[m])
            pre_all[tile(r, quarter), :] = (back * slope_all[tile(r, quarter), :]).astype(BF16)

        send_weights(0)
        pass_on(1, 0)
        pass_on(1, 1)
        in_spread = Spread(slab, in_s, in_a, in_i)

        @pl.when(s != 0)
        def _():
            copy(g_new.at[:, 0:width], slab(m), ix_s, ix_r, {"section": 0}).wait_recv()

        in_spread.start()

        total = i_tx[d].astype(F32)
        for p in near:
            copy(i_tx.at[p], i_rx.at[p], im_s, im_r.at[p], {"dp": p}).wait_recv()
            total = total + i_rx[p].astype(F32)
        unit, length = unit_rows(image[mine_half, :])
        image_out[mine_half, :] = unit_backward(unit, length, mult * total).astype(BF16)
        for t in others(s, n_sec):
            copy(image_out.at[mine_half, :], image_out.at[mine_half, :], io_s, io_r.at[s], {"section": t}).start()

        pass_on(0, 0)
        in_spread.relay()
        in_spread.finish()
        pass_on(0, 1)

        for t in sources(s, n_sec):
            part = image_out.at[tile(t, half), :]
            copy(part, part, io_s, io_r.at[t], {"section": t}).wait_recv()

        wait_sent(cols.at[pl.ds(0, (n_dp - 1) * half), :], gat_s)
        wait_sent(col_rx.at[pl.ds(0, n_dp - 1)], cs_s)
        wait_sent(row_rx.at[pl.ds(0, n_sec * n_mp - 1)], rs_s)
        wait_sent(wi_all.at[pl.ds(0, n_mp - 1)], wi_s)
        wait_sent(wo_all.at[pl.ds(0, n_mp - 1)], wo_s)
        if cores > 1:
            wait_sent(a_tx, a_s)
        if chips > 1:
            wait_sent(b_tx.at[pl.ds(0, chips - 1)], b_s)
        wait_sent(g_all.at[pl.ds(0, n_mp - 1)], g_s)
        wait_sent(i_tx.at[pl.ds(0, n_dp - 1)], im_s)
        wait_sent(input_out.at[pl.ds(0, (n_mp - 1) * quarter), :], in_s)
        wait_sent(image_out.at[pl.ds(0, (n_sec - 1) * half), :], io_s)

        @pl.when(s != last)
        def _():
            wait_sent(c_tx, c_s)

        @pl.when(s > 0)
        def _():
            wait_sent(g_new, x_s)

        @pl.when(s == 0)
        def _():
            wait_sent(g_new.at[:, pl.ds(0, (n_sec - 1) * width)], ix_s)

        for which, out in ((1, second_out), (0, first_out)):
            out[...] = w_tx[d, which].astype(F32)

            for p in [0, 1] if via_hub else near:
                copy(w_rx.at[p, which], w_rx.at[p, which], w_s, w_r.at[which, p], {"dp": mate}).wait_recv()
                out[...] += w_rx[p, which].astype(F32)
        wait_sent(w_tx.at[pl.ds(0, n_dp - 1)], w_s)

    return kernel


def store(image, inputs, first, second, image_out, input_out, first_out, second_out, sems):
    copies = [
        pltpu.make_async_copy(image, image_out, sems.at[0]),
        pltpu.make_async_copy(inputs, input_out, sems.at[1]),
        pltpu.make_async_copy(first, first_out.at[0], sems.at[2]),
        pltpu.make_async_copy(second, second_out.at[0], sems.at[3]),
    ]
    for c in copies:
        c.start()
    for c in copies:
        c.wait()


def solution(mesh):
    n_sec, n_dp, n_mp = mesh.shape["section"], mesh.shape["dp"], mesh.shape["mp"]

    def body(text, image, scale, hidden, w_in, w_out):
        rows, feats = text.shape
        own = image.shape[0]
        hid = w_in.shape[2]
        quarter, half, share = rows // n_mp, own // n_sec, feats // n_dp
        columns = half * n_dp
        cores = 2 if n_mp % 2 == 0 else 1
        chips = n_mp // cores
        dma = pltpu.SemaphoreType.DMA
        vmem = pl.BlockSpec(memory_space=pltpu.VMEM)
        hbm = pl.BlockSpec(memory_space=pltpu.HBM)
        out = pl.pallas_call(
            make_kernel(n_sec, n_dp, n_mp),
            out_shape=(
                pltpu.VMEM((own, feats), BF16),
                pltpu.VMEM((rows, feats // n_sec), BF16),
                pltpu.VMEM((share, hid), F32),
                pltpu.VMEM((share, hid), F32),
            ),
            in_specs=[hbm, hbm, pl.BlockSpec(memory_space=pltpu.SMEM), hbm, hbm, hbm],
            out_specs=(vmem,) * 4,
            scratch_shapes=[
                pltpu.VMEM((rows, feats), BF16),
                pltpu.VMEM((own, feats), BF16),
                pltpu.VMEM((rows, feats), BF16),
                pltpu.VMEM((rows, feats), BF16),
                pltpu.VMEM((columns, feats), BF16),
                pltpu.VMEM((rows, columns), F32),
                pltpu.VMEM((rows, columns), BF16),
                pltpu.VMEM((rows, LANES), F32),
                pltpu.VMEM((rows, LANES), F32),
                pltpu.VMEM((n_mp, quarter, LANES), F32),
                pltpu.VMEM((2 * n_mp, quarter), F32),
                pltpu.VMEM((n_sec * n_mp, 2 * n_mp, quarter), F32),
                pltpu.VMEM((2 * n_dp, half), F32),
                pltpu.VMEM((n_dp, 2 * n_dp, half), F32),
                pltpu.VMEM((feats, hid), BF16),
                pltpu.VMEM((hid, feats), BF16),
                pltpu.VMEM((n_mp, hid, feats), BF16),
                pltpu.VMEM((n_mp, feats, hid), BF16),
                pltpu.VMEM((n_mp, quarter, hid), F32),
                pltpu.VMEM((rows, hid), F32),
                pltpu.VMEM((rows, hid), BF16),
                pltpu.VMEM((rows, hid), BF16),
                pltpu.VMEM((quarter // PIECES * GROUP, n_mp * hid), BF16),
                pltpu.VMEM((chips, quarter, feats), BF16),
                pltpu.VMEM((chips, quarter, feats), BF16),
                pltpu.VMEM((chips, quarter, feats), BF16),
                pltpu.VMEM((chips, quarter, feats), BF16),
                pltpu.VMEM((quarter, feats), BF16),
                pltpu.VMEM((n_sec, quarter, feats), BF16),
                pltpu.VMEM((quarter, feats), F32),
                pltpu.VMEM((n_mp, quarter, feats), BF16),
                pltpu.VMEM((quarter, feats), BF16),
                pltpu.VMEM((n_dp, 2, share, hid), BF16),
                pltpu.VMEM((n_dp, 2, share, hid), BF16),
                pltpu.VMEM((2, 2, share, hid), BF16),
                pltpu.VMEM((n_dp, half, feats), BF16),
                pltpu.VMEM((n_dp, half, feats), BF16),
                dma((5,)),
                dma, dma((n_dp,)),
                dma, dma((n_dp,)),
                dma, dma((n_sec * n_mp,)),
                dma, dma((2, chips)), dma((2, chips)),
                dma, dma((chips,)), dma, dma((chips,)), dma((chips, 2)),
                dma, dma((chips,)),
                dma, dma((chips, PIECES)),
                dma, dma((n_sec, PIECES)),
                dma, dma((chips, PIECES)), dma((chips, PIECES // GROUP)),
                dma, dma((PIECES,)),
                dma, dma((chips,)), dma((chips,)),
                dma, dma,
                dma, dma((2, 2 if n_dp == 4 else n_dp)), dma((2, 2)),
                dma, dma((n_dp,)),
                dma, dma((n_sec,)),
            ],
            compiler_params=pltpu.CompilerParams(
                collective_id=0, has_side_effects=True, vmem_limit_bytes=50000000
            ),
        )(*(pltpu.with_memory_space_constraint(x, pltpu.HBM) for x in (text, image)), scale,
          *(pltpu.with_memory_space_constraint(x[0], pltpu.HBM) for x in (hidden, w_in, w_out)))
        return tuple(
            pl.pallas_call(
                store,
                out_shape=(
                    jax.ShapeDtypeStruct((own, feats), BF16),
                    jax.ShapeDtypeStruct((rows, feats // n_sec), BF16),
                    jax.ShapeDtypeStruct((1, share, hid), F32),
                    jax.ShapeDtypeStruct((1, share, hid), F32),
                ),
                in_specs=[vmem] * 4,
                out_specs=(hbm,) * 4,
                scratch_shapes=[dma((4,))],
                compiler_params=pltpu.CompilerParams(has_side_effects=True),
            )(*(pltpu.with_memory_space_constraint(x, pltpu.VMEM) for x in out))
        )

    return jax.shard_map(
        body,
        mesh=mesh,
        in_specs=(
            P("dp", None),
            P(("dp", "mp"), None),
            P(),
            P("section", "dp", None),
            P("section", None, "mp"),
            P("section", "mp", None),
        ),
        out_specs=(
            P(("dp", "mp"), None),
            P("dp", "section"),
            P("section", "dp", "mp"),
            P("section", "dp", "mp"),
        ),
        check_vma=False,
    )
```

time: 71.5 us -> 64.8 us (0.906)
  Pallas kernels: 70.1 us -> 63.3 us
    pallas_call x1, Pallas kernels: 69 us -> 62.3 us  [body(): pl.pallas_call(make_kernel(n_sec, n_dp, n_mp), out_shape=(pltpu.VMEM((own...]
where the time goes in v3:
time: 64.8 us; the launch traced here: 64.6 us
  Pallas kernels  63.3 us (98%)
  between operations  1.29 us (2%)
    pallas_call x1, Pallas kernels, body(): pl.pallas_call(make_kernel(n_sec, n_dp, n_mp), out_shape=(pltpu.VMEM((own...  62.3 us

profile of v3, /device:TPU:0, one launch (start us, length us, event | category | flops | bytes accessed | tf_op | source)
XLA Modules:
  0.0 64.6 jit_solution(7468243499555717819)
XLA Ops:
  1.3 62.3 %shard_map.93 = (bf16[256,512]{1,0:T(8,128)(2,1)S(1)}, bf16[1024,256]{1,0:T(8,128)(2,1)S(1)}, f32[128,512]{1,0:T(8,128)S(1)}, f32[128,512]{1,0:T(8,128)S(1)}) custom-call(bf16[1024,512]{1,0:T(8,128)(2,1)} %text_in.1, bf16[256,512]{1,0:T(8,128)(2,1)} %image_in.1, f32[1]{0:T(128)S(6)} %copy.10.scale_ref, bf16[1024,512]{1,0:T(8,128)(2,1)} %bitcast.3, ...), custom_call_target="tpu_custom_call" | custom-call | tf_op jit(solution)/shard_map/pallas_call | solution.py:657
  63.5 1.1 %shard_map.94 = (bf16[256,512]{1,0:T(8,128)(2,1)}, bf16[1024,256]{1,0:T(8,128)(2,1)}, f32[1,128,512]{2,1,0:T(8,128)}, f32[1,128,512]{2,1,0:T(8,128)}) custom-call(bf16[256,512]{1,0:T(8,128)(2,1)S(1)} %get-tuple-element.8.image, bf16[1024,256]{1,0:T(8,128)(2,1)S(1)} %get-tuple-element.9.inputs, f32[128,512]{1,0:T(8,128)S(1)} %get-tuple-element.10.first, ...), custom_call_target="tpu_custom_call" | custom-call | tf_op jit(solution)/shard_map/pallas_call | solution.py:728

commit v4 on v3

--- a/solution.py
+++ b/solution.py
@@ -62,10 +62,10 @@
         text_low, cols, scores, sgrad, row_max, row_sum, row_lse, row_st, row_rx, col_st, col_rx,
         raw_in, raw_out, wi_all, wo_all, slope_own, slope_all, act_all, pre_all, grad_own,
         a_tx, a_rx, b_tx, b_rx, c_tx, c_rx, t_acc, g_all, g_new,
-        w_tx, w_rx, w_via, i_tx, i_rx,
+        w_acc, w_tx, w_rx, w_via, w_side, i_tx, i_rx,
         ld, gat_s, gat_r, cs_s, cs_r, rs_s, rs_r, wi_s, wi_a, wi_i,
         wo_s, yo_r, so_r, zo_r, fo_r, a_s, a_r, b_s, b_r, c_s, c_r, g_s, ga_r, gi_r, x_s, x_r,
-        in_s, in_a, in_i, ix_s, ix_r, w_s, w_r, v_r, im_s, im_r, io_s, io_r,
+        in_s, in_a, in_i, ix_s, ix_r, w_s, w_r, v_r, sd_s, sd_r, im_s, im_r, io_s, io_r,
     ):
         s = lax.axis_index("section")
         d = lax.axis_index("dp")
@@ -89,7 +89,7 @@
                 device_id=where, device_id_type=MESH,
             )
 
-        def wait_sent(ref, sem):
+        def wait_all(ref, sem):
             pltpu.make_async_copy(ref, ref, sem).wait()
 
         def others(mine, count):
@@ -108,6 +108,11 @@
             pl.semaphore_signal(barrier, inc=1, device_id={"section": t, "mp": p}, device_id_type=MESH)
         for p in near:
             pl.semaphore_signal(barrier, inc=1, device_id={"dp": p}, device_id_type=MESH)
+        via_hub = n_dp == 4
+        by_side = via_hub and n_sec == 2
+        mate = d + 1 - 2 * lax.rem(d, 2)
+        if by_side:
+            pl.semaphore_signal(barrier, inc=1, device_id={"section": 1 - s, "dp": mate}, device_id_type=MESH)
 
         loads = [
             pltpu.make_async_copy(image_in, image, ld.at[0]),
@@ -123,7 +128,7 @@
         loads[0].wait()
         own_unit, _ = unit_rows(image[mine_half, :])
         cols[tile(d, half), :] = own_unit.astype(BF16)
-        pl.semaphore_wait(barrier, len(plane) + n_dp - 1)
+        pl.semaphore_wait(barrier, len(plane) + n_dp - 1 + (1 if by_side else 0))
 
         for p in far:
             copy(cols.at[tile(d, half), :], cols.at[tile(d, half), :], gat_s, gat_r.at[d], {"dp": p}).start()
@@ -136,15 +141,15 @@
                 copy(self.slot(index), self.slot(index), self.send, recv, {"mp": to}).start()
 
             def start(self):
-                for q in others(chip, chips):
-                    self.push(m, self.across.at[chip], q * cores + core)
+                for k, q in enumerate(others(chip, chips)):
+                    self.push(m, self.across.at[k], q * cores + core)
                 for e in others(core, cores):
                     self.push(m, self.inside.at[chip], chip * cores + e)
 
             def relay(self):
-                for q in sources(chip, chips):
+                for k, q in enumerate(sources(chip, chips)):
                     index = q * cores + core
-                    copy(self.slot(index), self.slot(index), self.send, self.across.at[q], {"mp": index}).wait_recv()
+                    copy(self.slot(index), self.slot(index), self.send, self.across.at[k], {"mp": index}).wait_recv()
                     for e in others(core, cores):
                         self.push(index, self.inside.at[q], chip * cores + e)
 
@@ -166,8 +171,8 @@
         def wo_push(ref, recv, to):
             copy(ref, ref, wo_s, recv, to).start()
 
-        for q in others(chip, chips):
-            wo_push(wo_part(m, side), yo_r.at[chip], {"mp": q * cores + core})
+        for k, q in enumerate(others(chip, chips)):
+            wo_push(wo_part(m, side), yo_r.at[k], {"mp": q * cores + core})
         for e in others(core, cores):
             wo_push(wo_all.at[m], so_r, {"mp": chip * cores + e})
 
@@ -181,32 +186,32 @@
         wi_spread[0].start()
 
         def wo_across():
-            for q in sources(chip, chips):
+            for k, q in enumerate(sources(chip, chips)):
                 index = q * cores + core
                 at = wo_part(index, side)
-                copy(at, at, wo_s, yo_r.at[q], {"mp": index}).wait_recv()
+                copy(at, at, wo_s, yo_r.at[k], {"mp": index}).wait_recv()
                 if pairs == 2:
-                    wo_push(at, zo_r.at[q], {"dp": d + 1 - 2 * side})
+                    wo_push(at, zo_r.at[k], {"dp": d + 1 - 2 * side})
                 for e in others(core, cores):
-                    wo_push(at, fo_r.at[q, 0], {"mp": chip * cores + e})
+                    wo_push(at, fo_r.at[k, 0], {"mp": chip * cores + e})
 
         def wo_along():
-            for q in sources(chip, chips):
+            for k, q in enumerate(sources(chip, chips)):
                 at = wo_part(q * cores + core, 1 - side)
                 if pairs == 2:
-                    copy(at, at, wo_s, zo_r.at[q], {"dp": d + 1 - 2 * side}).wait_recv()
+                    copy(at, at, wo_s, zo_r.at[k], {"dp": d + 1 - 2 * side}).wait_recv()
                     for e in others(core, cores):
-                        wo_push(at, fo_r.at[q, 1], {"mp": chip * cores + e})
+                        wo_push(at, fo_r.at[k, 1], {"mp": chip * cores + e})
 
         def wo_finish():
             for e in sources(core, cores):
                 to = {"mp": chip * cores + e}
                 own_block = wo_all.at[chip * cores + e]
                 copy(own_block, own_block, wo_s, so_r, to).wait_recv()
-                for q in sources(chip, chips):
+                for i, q in enumerate(sources(chip, chips)):
                     for k in range(pairs):
                         at = wo_part(q * cores + e, side if k == 0 else 1 - side)
-                        copy(at, at, wo_s, fo_r.at[q, k], to).wait_recv()
+                        copy(at, at, wo_s, fo_r.at[i, k], to).wait_recv()
 
         loads[3].wait()
 
@@ -276,7 +281,7 @@
 
         col_rx[d] = col_st[...]
         for p in far:
-            copy(col_st, col_rx.at[d], cs_s, cs_r.at[d], {"dp": p}).start()
+            copy(col_st, col_rx.at[d], cs_s, cs_r, {"dp": p}).start()
 
         wo_across()
         block_rows(far[0])
@@ -293,7 +298,7 @@
         here = s * n_mp + m
         row_rx[here] = row_st[...]
         for k, (t, p) in enumerate(plane):
-            copy(row_st, row_rx.at[here], rs_s, rs_r.at[here], {"section": t, "mp": p}).start()
+            copy(row_st, row_rx.at[here], rs_s, rs_r, {"section": t, "mp": p}).start()
 
         wi_spread[1].start()
         wi_spread[0].relay()
@@ -307,11 +312,9 @@
                 acc = acc + rx[k, n : 2 * n, :] * jnp.exp(rx[k, 0:n, :] - peak)
             return peak + jnp.log(acc)
 
-        for p in near:
-            copy(col_st, col_rx.at[p], cs_s, cs_r.at[p], {"dp": p}).wait_recv()
+        wait_all(col_rx.at[pl.ds(0, n_dp - 1)], cs_r)
         col_lse = merge(col_rx, n_dp, n_dp)
-        for t, p in plane:
-            copy(row_st, row_rx.at[t * n_mp + p], rs_s, rs_r.at[t * n_mp + p], {"section": t, "mp": p}).wait_recv()
+        wait_all(row_rx.at[pl.ds(0, n_sec * n_mp - 1)], rs_r)
         merged = merge(row_rx, n_sec * n_mp, n_mp)
         for r in range(n_mp):
             row_lse[r] = jnp.broadcast_to(merged[r : r + 1, :], (LANES, quarter)).T
@@ -357,14 +360,14 @@
                 copy(a_tx.at[q], a_rx.at[q], a_s, a_r.at[q], {"mp": chip * cores + e}).wait_recv()
                 t_acc[...] += a_rx[q].astype(F32)
 
-        for q in others(chip, chips):
+        for i, q in enumerate(others(chip, chips)):
             for_sibling(q)
             score_rows(q * cores + core)
             t_acc[...] = text_part(q * cores + core)
             from_sibling(q)
             b_tx[q] = t_acc[...].astype(BF16)
             for k in range(PIECES):
-                copy(b_tx.at[q, rows_of(k), :], b_rx.at[chip, rows_of(k), :], b_s, b_r.at[chip, k],
+                copy(b_tx.at[q, rows_of(k), :], b_rx.at[i, rows_of(k), :], b_s, b_r.at[i, k],
                      {"mp": q * cores + core}).start()
         for_sibling(chip)
         score_rows(m)
@@ -376,7 +379,7 @@
 
         for p in far:
             i_tx[p] = image_part(p).astype(BF16)
-            copy(i_tx.at[p], i_rx.at[d], im_s, im_r.at[d], {"dp": p}).start()
+            copy(i_tx.at[p], i_rx.at[d], im_s, im_r, {"dp": p}).start()
         i_tx[d] = image_part(d).astype(BF16)
 
         from_sibling(chip)
@@ -386,10 +389,10 @@
 
         def gather_sum(k):
             total = t_acc[rows_of(k), :]
-            for q in sources(chip, chips):
-                copy(b_tx.at[q, rows_of(k), :], b_rx.at[q, rows_of(k), :], b_s, b_r.at[q, k],
+            for i, q in enumerate(sources(chip, chips)):
+                copy(b_tx.at[q, rows_of(k), :], b_rx.at[i, rows_of(k), :], b_s, b_r.at[i, k],
                      {"mp": q * cores + core}).wait_recv()
-                total = total + b_rx[q, rows_of(k), :].astype(F32)
+                total = total + b_rx[i, rows_of(k), :].astype(F32)
             return total
 
         def to_last(k):
@@ -446,8 +449,8 @@
                     copy(g_new.at[rows_of(k), :], g_all.at[m, rows_of(k), :], x_s, x_r.at[k],
                          {"section": s + 1}).wait_recv()
 
-                for q in others(chip, chips):
-                    g_push(k, m, ga_r.at[chip, k], q * cores + core)
+                for j, q in enumerate(others(chip, chips)):
+                    g_push(k, m, ga_r.at[j, k], q * cores + core)
 
             group = tile(i, GROUP * piece)
             for e in others(core, cores):
@@ -465,16 +468,37 @@
                 for k in range(GROUP):
                     to_below(i * GROUP + k).start()
 
-        for i in range(PIECES // GROUP):
-            group = pl.ds(i * GROUP * piece, GROUP * piece)
-            for q in sources(chip, chips):
+        groups = PIECES // GROUP
+
+        def group_of(i):
+            return pl.ds(i * GROUP * piece, GROUP * piece)
+
+        def relay_group(i):
+            for j, q in enumerate(sources(chip, chips)):
                 index = q * cores + core
                 for k in range(i * GROUP, (i + 1) * GROUP):
                     slot = g_all.at[index, rows_of(k), :]
-                    copy(slot, slot, g_s, ga_r.at[q, k], {"mp": index}).wait_recv()
-                slot = g_all.at[index, group, :]
+                    copy(slot, slot, g_s, ga_r.at[j, k], {"mp": index}).wait_recv()
+                slot = g_all.at[index, group_of(i), :]
                 for e in others(core, cores):
                     copy(slot, slot, g_s, gi_r.at[q, i], {"mp": chip * cores + e}).start()
+
+        def sibling_groups(q):
+            for i in range(groups):
+                for e in sources(core, cores):
+                    slot = g_all.at[q * cores + e, group_of(i), :]
+                    copy(slot, slot, g_s, gi_r.at[q, i], {"mp": chip * cores + e}).wait_recv()
+
+        def chip_grad(q, at):
+            left = g_all[pl.ds(q * cores, cores), :, at]
+            return dot_tn(left.reshape(cores * quarter, left.shape[2]), act_all[tile(q, cores * quarter), :])
+
+        for i in range(groups - 2):
+            relay_group(i)
+        sibling_groups(chip)
+        relay_group(groups - 2)
+        w_acc[...] = chip_grad(chip, pl.ds(0, feats))
+        relay_group(groups - 1)
 
         def slab(k):
             return input_out.at[tile(k, quarter), :]
@@ -489,14 +513,9 @@
                 final(t).start()
             input_out[mine, :] = g_new[:, 0:width]
 
-        for i in range(PIECES // GROUP):
-            for e in sources(core, cores):
-                for q in range(chips):
-                    slot = g_all.at[q * cores + e, pl.ds(i * GROUP * piece, GROUP * piece), :]
-                    copy(slot, slot, g_s, gi_r.at[q, i], {"mp": chip * cores + e}).wait_recv()
-
-        via_hub = n_dp == 4
-        mate = d + 1 - 2 * lax.rem(d, 2)
+        for q in sources(chip, chips):
+            sibling_groups(q)
+
         low = d < n_dp // 2
         end = (d == 0) | (d == n_dp - 1)
         inner = jnp.logical_not(end)
@@ -504,15 +523,52 @@
 
         def weight_grad(which, at):
             if which == 1:
-                left = g_all[:, :, at]
-                return dot_tn(left.reshape(rows, left.shape[2]), act_all[...]).astype(BF16)
+                total = w_acc[at, :]
+                for q in sources(chip, chips):
+                    total = total + chip_grad(q, at)
+                return total.astype(BF16)
             return dot_tn(hidden[:, at], pre_all[...]).astype(BF16)
+
+        halves = [pl.ds(h * (share // 2), share // 2) for h in range(2)]
 
         def to_dp(which, p, slot):
             return copy(w_tx.at[p, which], w_rx.at[slot, which], w_s, w_r.at[which, slot], {"dp": p})
 
         def to_hub(which, k):
-            return copy(w_tx.at[cross[k], which], w_via.at[which, k], w_s, v_r.at[which, k], {"dp": mate})
+            return [
+                copy(w_tx.at[cross[k], which, at, :], w_via.at[which, k, at, :], w_s, v_r.at[which, k, h], {"dp": mate})
+                for h, at in enumerate(halves)
+            ]
+
+        def to_cross(which, k, h):
+            return copy(w_tx.at[cross[k], which, halves[h], :], w_rx.at[1, which, halves[h], :], w_s,
+                        w_r.at[which, 1 + h], {"dp": cross[k]})
+
+        def to_side():
+            return copy(w_tx.at[mate, 1], w_side, w_s, sd_r, {"section": 1})
+
+        def from_side():
+            return copy(w_side, w_rx.at[0, 1], sd_s, w_r.at[1, 0], {"section": 0, "dp": mate})
+
+        def last_weights():
+            if by_side:
+                pl.when(end & (s == 0))(lambda: to_dp(0, mate, 0).start())
+                pl.when(end & (s == 1))(lambda: to_dp(1, mate, 0).start())
+            elif via_hub:
+
+                @pl.when(end)
+                def _():
+                    to_dp(1, mate, 0).start()
+                    to_dp(0, mate, 0).start()
+
+        def side_weights():
+            if by_side:
+
+                @pl.when(end & (s == 1))
+                def _():
+                    to_side().wait_recv()
+                    from_side().start()
+                    to_dp(0, mate, 0).start()
 
         def send_weights(which):
             if via_hub:
@@ -521,7 +577,8 @@
 
                     @pl.when(end)
                     def _():
-                        to_hub(which, k).start()
+                        for c in to_hub(which, 0) if k == 0 else to_hub(1, 1) + to_hub(0, 1) if which == 0 else []:
+                            c.start()
 
                 w_tx[mate, which] = weight_grad(which, tile(mate, share))
 
@@ -529,12 +586,11 @@
                 def _():
                     to_dp(which, mate, 0).start()
 
-                if which == 0:
-
-                    @pl.when(end)
+                if by_side and which == 1:
+
+                    @pl.when(end & (s == 0))
                     def _():
-                        to_dp(1, mate, 0).start()
-                        to_dp(0, mate, 0).start()
+                        to_side().start()
 
                 w_tx[d, which] = weight_grad(which, tile(d, share))
             else:
@@ -544,15 +600,15 @@
                 for p in far:
                     to_dp(which, p, d).start()
 
-        def pass_on(which, k):
+        def pass_on(which, k, h):
             if via_hub:
 
                 @pl.when(inner)
                 def _():
-                    to_hub(which, k).wait_recv()
-                    both = w_tx[cross[k], which].astype(F32) + w_via[which, k].astype(F32)
-                    w_tx[cross[k], which] = both.astype(BF16)
-                    to_dp(which, cross[k], 1).start()
+                    to_hub(which, k)[h].wait_recv()
+                    both = w_tx[cross[k], which, halves[h], :].astype(F32) + w_via[which, k, halves[h], :].astype(F32)
+                    w_tx[cross[k], which, halves[h], :] = both.astype(BF16)
+                    to_cross(which, k, h).start()
 
         send_weights(1)
 
@@ -561,9 +617,12 @@
             back = dot_nn(g_all[r], wo_all[m])
             pre_all[tile(r, quarter), :] = (back * slope_all[tile(r, quarter), :]).astype(BF16)
 
+        pass_on(1, 0, 0)
         send_weights(0)
-        pass_on(1, 0)
-        pass_on(1, 1)
+        last_weights()
+        pass_on(1, 0, 1)
+        for h in range(2):
+            pass_on(0, 0, h)
         in_spread = Spread(slab, in_s, in_a, in_i)
 
         @pl.when(s != 0)
@@ -573,56 +632,61 @@
         in_spread.start()
 
         total = i_tx[d].astype(F32)
+        wait_all(i_rx.at[pl.ds(0, n_dp - 1)], im_r)
         for p in near:
-            copy(i_tx.at[p], i_rx.at[p], im_s, im_r.at[p], {"dp": p}).wait_recv()
             total = total + i_rx[p].astype(F32)
         unit, length = unit_rows(image[mine_half, :])
         image_out[mine_half, :] = unit_backward(unit, length, mult * total).astype(BF16)
         for t in others(s, n_sec):
-            copy(image_out.at[mine_half, :], image_out.at[mine_half, :], io_s, io_r.at[s], {"section": t}).start()
-
-        pass_on(0, 0)
+            copy(image_out.at[mine_half, :], image_out.at[mine_half, :], io_s, io_r, {"section": t}).start()
+
+        side_weights()
+        for which in (1, 0):
+            for h in range(2):
+                pass_on(which, 1, h)
         in_spread.relay()
         in_spread.finish()
-        pass_on(0, 1)
-
-        for t in sources(s, n_sec):
-            part = image_out.at[tile(t, half), :]
-            copy(part, part, io_s, io_r.at[t], {"section": t}).wait_recv()
-
-        wait_sent(cols.at[pl.ds(0, (n_dp - 1) * half), :], gat_s)
-        wait_sent(col_rx.at[pl.ds(0, n_dp - 1)], cs_s)
-        wait_sent(row_rx.at[pl.ds(0, n_sec * n_mp - 1)], rs_s)
-        wait_sent(wi_all.at[pl.ds(0, n_mp - 1)], wi_s)
-        wait_sent(wo_all.at[pl.ds(0, n_mp - 1)], wo_s)
+
+        wait_all(image_out.at[pl.ds(0, (n_sec - 1) * half), :], io_r)
+
+        wait_all(cols.at[pl.ds(0, (n_dp - 1) * half), :], gat_s)
+        wait_all(col_rx.at[pl.ds(0, n_dp - 1)], cs_s)
+        wait_all(row_rx.at[pl.ds(0, n_sec * n_mp - 1)], rs_s)
+        wait_all(wi_all.at[pl.ds(0, n_mp - 1)], wi_s)
+        wait_all(wo_all.at[pl.ds(0, n_mp - 1)], wo_s)
         if cores > 1:
-            wait_sent(a_tx, a_s)
+            wait_all(a_tx, a_s)
         if chips > 1:
-            wait_sent(b_tx.at[pl.ds(0, chips - 1)], b_s)
-        wait_sent(g_all.at[pl.ds(0, n_mp - 1)], g_s)
-        wait_sent(i_tx.at[pl.ds(0, n_dp - 1)], im_s)
-        wait_sent(input_out.at[pl.ds(0, (n_mp - 1) * quarter), :], in_s)
-        wait_sent(image_out.at[pl.ds(0, (n_sec - 1) * half), :], io_s)
+            wait_all(b_tx.at[pl.ds(0, chips - 1)], b_s)
+        wait_all(g_all.at[pl.ds(0, n_mp - 1)], g_s)
+        wait_all(i_tx.at[pl.ds(0, n_dp - 1)], im_s)
+        wait_all(input_out.at[pl.ds(0, (n_mp - 1) * quarter), :], in_s)
+        wait_all(image_out.at[pl.ds(0, (n_sec - 1) * half), :], io_s)
 
         @pl.when(s != last)
         def _():
-            wait_sent(c_tx, c_s)
+            wait_all(c_tx, c_s)
 
         @pl.when(s > 0)
         def _():
-            wait_sent(g_new, x_s)
+            wait_all(g_new, x_s)
 
         @pl.when(s == 0)
         def _():
-            wait_sent(g_new.at[:, pl.ds(0, (n_sec - 1) * width)], ix_s)
+            wait_all(g_new.at[:, pl.ds(0, (n_sec - 1) * width)], ix_s)
 
         for which, out in ((1, second_out), (0, first_out)):
             out[...] = w_tx[d, which].astype(F32)
 
-            for p in [0, 1] if via_hub else near:
+            for p in [0] if via_hub else near:
                 copy(w_rx.at[p, which], w_rx.at[p, which], w_s, w_r.at[which, p], {"dp": mate}).wait_recv()
                 out[...] += w_rx[p, which].astype(F32)
-        wait_sent(w_tx.at[pl.ds(0, n_dp - 1)], w_s)
+            for h, at in enumerate(halves if via_hub else []):
+                to_cross(which, 0, h).wait_recv()
+                out[at, :] += w_rx[1, which, at, :].astype(F32)
+        wait_all(w_tx.at[pl.ds(0, n_dp - 1)], w_s)
+        if by_side:
+            pl.when(end & (s == 1))(lambda: wait_all(w_side, sd_s))
 
     return kernel
 
@@ -651,6 +715,7 @@
         columns = half * n_dp
         cores = 2 if n_mp % 2 == 0 else 1
         chips = n_mp // cores
+        away = max(chips - 1, 1)
         dma = pltpu.SemaphoreType.DMA
         vmem = pl.BlockSpec(memory_space=pltpu.VMEM)
         hbm = pl.BlockSpec(memory_space=pltpu.HBM)
@@ -697,27 +762,29 @@
                 pltpu.VMEM((quarter, feats), F32),
                 pltpu.VMEM((n_mp, quarter, feats), BF16),
                 pltpu.VMEM((quarter, feats), BF16),
+                pltpu.VMEM((feats, hid), F32),
                 pltpu.VMEM((n_dp, 2, share, hid), BF16),
                 pltpu.VMEM((n_dp, 2, share, hid), BF16),
                 pltpu.VMEM((2, 2, share, hid), BF16),
+                pltpu.VMEM((share, hid), BF16),
                 pltpu.VMEM((n_dp, half, feats), BF16),
                 pltpu.VMEM((n_dp, half, feats), BF16),
                 dma((5,)),
                 dma, dma((n_dp,)),
-                dma, dma((n_dp,)),
-                dma, dma((n_sec * n_mp,)),
-                dma, dma((2, chips)), dma((2, chips)),
-                dma, dma((chips,)), dma, dma((chips,)), dma((chips, 2)),
+                dma, dma,
+                dma, dma,
+                dma, dma((2, away)), dma((2, chips)),
+                dma, dma((away,)), dma, dma((away,)), dma((away, 2)),
                 dma, dma((chips,)),
-                dma, dma((chips, PIECES)),
-                dma, dma((n_sec, PIECES)),
-                dma, dma((chips, PIECES)), dma((chips, PIECES // GROUP)),
+                dma, dma((away, PIECES)),
+                dma, dma((n_sec - 1, PIECES)),
+                dma, dma((away, PIECES)), dma((chips, PIECES // GROUP)),
                 dma, dma((PIECES,)),
-                dma, dma((chips,)), dma((chips,)),
+                dma, dma((away,)), dma((chips,)),
                 dma, dma,
-                dma, dma((2, 2 if n_dp == 4 else n_dp)), dma((2, 2)),
-                dma, dma((n_dp,)),
-                dma, dma((n_sec,)),
+                dma, dma((2, 3 if n_dp == 4 else n_dp)), dma((2, 2, 2)), dma, dma,
+                dma, dma,
+                dma, dma,
             ],
             compiler_params=pltpu.CompilerParams(
                 collective_id=0, has_side_effects=True, vmem_limit_bytes=50000000

time: 64.8 us -> 62.7 us (0.968)
  Pallas kernels: 63.3 us -> 60.8 us
    pallas_call x1, Pallas kernels: 62.3 us -> 59.7 us  [body(): pl.pallas_call(make_kernel(n_sec, n_dp, n_mp), out_shape=(pltpu.VMEM((own...]
where the time goes in v4:
time: 62.7 us; the launch traced here: 62.1 us
  Pallas kernels  60.8 us (97%)
  between operations  1.29 us (2%)
    pallas_call x1, Pallas kernels, body(): pl.pallas_call(make_kernel(n_sec, n_dp, n_mp), out_shape=(pltpu.VMEM((own...  59.7 us

profile of v4, /device:TPU:0, one launch (start us, length us, event | category | flops | bytes accessed | tf_op | source)
XLA Modules:
  0.0 62.1 jit_solution(8212233925824814304)
XLA Ops:
  1.3 59.7 %shard_map.93 = (bf16[256,512]{1,0:T(8,128)(2,1)S(1)}, bf16[1024,256]{1,0:T(8,128)(2,1)S(1)}, f32[128,512]{1,0:T(8,128)S(1)}, f32[128,512]{1,0:T(8,128)S(1)}) custom-call(bf16[1024,512]{1,0:T(8,128)(2,1)} %text_in.1, bf16[256,512]{1,0:T(8,128)(2,1)} %image_in.1, f32[1]{0:T(128)S(6)} %copy.10.scale_ref, bf16[1024,512]{1,0:T(8,128)(2,1)} %bitcast.3, ...), custom_call_target="tpu_custom_call" | custom-call | tf_op jit(solution)/shard_map/pallas_call | solution.py:722
  61.0 1.1 %shard_map.94 = (bf16[256,512]{1,0:T(8,128)(2,1)}, bf16[1024,256]{1,0:T(8,128)(2,1)}, f32[1,128,512]{2,1,0:T(8,128)}, f32[1,128,512]{2,1,0:T(8,128)}) custom-call(bf16[256,512]{1,0:T(8,128)(2,1)S(1)} %get-tuple-element.8.image, bf16[1024,256]{1,0:T(8,128)(2,1)S(1)} %get-tuple-element.9.inputs, f32[128,512]{1,0:T(8,128)S(1)} %get-tuple-element.10.first, ...), custom_call_target="tpu_custom_call" | custom-call | tf_op jit(solution)/shard_map/pallas_call | solution.py:795

commit v5 on v4

--- a/solution.py
+++ b/solution.py
@@ -312,12 +312,13 @@
                 acc = acc + rx[k, n : 2 * n, :] * jnp.exp(rx[k, 0:n, :] - peak)
             return peak + jnp.log(acc)
 
-        wait_all(col_rx.at[pl.ds(0, n_dp - 1)], cs_r)
-        col_lse = merge(col_rx, n_dp, n_dp)
         wait_all(row_rx.at[pl.ds(0, n_sec * n_mp - 1)], rs_r)
         merged = merge(row_rx, n_sec * n_mp, n_mp)
         for r in range(n_mp):
             row_lse[r] = jnp.broadcast_to(merged[r : r + 1, :], (LANES, quarter)).T
+
+        wait_all(col_rx.at[pl.ds(0, n_dp - 1)], cs_r)
+        col_lse = merge(col_rx, n_dp, n_dp)
 
         def score_rows(r):
             line = row_lse[r]
@@ -572,19 +573,20 @@
 
         def send_weights(which):
             if via_hub:
-                for k in range(2):
-                    w_tx[cross[k], which] = weight_grad(which, tile(cross[k], share))
+                turn = [jnp.where(end, cross[0], mate), jnp.where(end, cross[1], cross[0]), jnp.where(end, mate, cross[1])]
+                for k, p in enumerate(turn):
+                    w_tx[p, which] = weight_grad(which, tile(p, share))
 
                     @pl.when(end)
                     def _():
-                        for c in to_hub(which, 0) if k == 0 else to_hub(1, 1) + to_hub(0, 1) if which == 0 else []:
+                        for c in to_hub(which, 0) if k == 0 else to_hub(1, 1) + to_hub(0, 1) if k + which == 1 else []:
                             c.start()
 
-                w_tx[mate, which] = weight_grad(which, tile(mate, share))
-
-                @pl.when(inner)
-                def _():
-                    to_dp(which, mate, 0).start()
+                    if k == 0:
+
+                        @pl.when(inner)
+                        def _():
+                            to_dp(which, mate, 0).start()
 
                 if by_side and which == 1:
 

time: 62.7 us -> 62.5 us (level)
  the two profiles are of different devices: /device:TPU:0 before, /device:TPU:9 now
where the time goes in v5:
time: 62.5 us; the launch traced here: 62.4 us
  Pallas kernels  61.1 us (98%)
  between operations  1.29 us (2%)
    pallas_call x1, Pallas kernels, body(): pl.pallas_call(make_kernel(n_sec, n_dp, n_mp), out_shape=(pltpu.VMEM((own...  60 us

profile of v5, /device:TPU:9, one launch (start us, length us, event | category | flops | bytes accessed | tf_op | source)
XLA Modules:
  0.0 62.4 jit_solution(5956521637164730336)
XLA Ops:
  1.3 60.0 %shard_map.93 = (bf16[256,512]{1,0:T(8,128)(2,1)S(1)}, bf16[1024,256]{1,0:T(8,128)(2,1)S(1)}, f32[128,512]{1,0:T(8,128)S(1)}, f32[128,512]{1,0:T(8,128)S(1)}) custom-call(bf16[1024,512]{1,0:T(8,128)(2,1)} %text_in.1, bf16[256,512]{1,0:T(8,128)(2,1)} %image_in.1, f32[1]{0:T(128)S(6)} %copy.10.scale_ref, bf16[1024,512]{1,0:T(8,128)(2,1)} %bitcast.3, ...), custom_call_target="tpu_custom_call" | custom-call | tf_op jit(solution)/shard_map/pallas_call | solution.py:724
  61.3 1.1 %shard_map.94 = (bf16[256,512]{1,0:T(8,128)(2,1)}, bf16[1024,256]{1,0:T(8,128)(2,1)}, f32[1,128,512]{2,1,0:T(8,128)}, f32[1,128,512]{2,1,0:T(8,128)}) custom-call(bf16[256,512]{1,0:T(8,128)(2,1)S(1)} %get-tuple-element.8.image, bf16[1024,256]{1,0:T(8,128)(2,1)S(1)} %get-tuple-element.9.inputs, f32[128,512]{1,0:T(8,128)S(1)} %get-tuple-element.10.first, ...), custom_call_target="tpu_custom_call" | custom-call | tf_op jit(solution)/shard_map/pallas_call | solution.py:797

commit v6 on v5

--- a/solution.py
+++ b/solution.py
@@ -64,7 +64,7 @@
         a_tx, a_rx, b_tx, b_rx, c_tx, c_rx, t_acc, g_all, g_new,
         w_acc, w_tx, w_rx, w_via, w_side, i_tx, i_rx,
         ld, gat_s, gat_r, cs_s, cs_r, rs_s, rs_r, wi_s, wi_a, wi_i,
-        wo_s, yo_r, so_r, zo_r, fo_r, a_s, a_r, b_s, b_r, c_s, c_r, g_s, ga_r, gi_r, x_s, x_r,
+        wo_s, yo_r, so_r, zo_r, fo_r, a_s, a_r, b_s, b_r, c_s, c_r, g_s, ga_r, gi_r, x_s,
         in_s, in_a, in_i, ix_s, ix_r, w_s, w_r, v_r, sd_s, sd_r, im_s, im_r, io_s, io_r,
     ):
         s = lax.axis_index("section")
@@ -401,7 +401,7 @@
                         {"section": last})
 
         def to_below(k):
-            return copy(g_new.at[rows_of(k), :], g_all.at[m, rows_of(k), :], x_s, x_r.at[k],
+            return copy(g_new.at[rows_of(k), :], g_all.at[m, rows_of(k), :], x_s, c_r.at[0, k],
                         {"section": s - 1})
 
         @pl.when(s != last)
@@ -447,7 +447,7 @@
 
                 @pl.when(s != last)
                 def _():
-                    copy(g_new.at[rows_of(k), :], g_all.at[m, rows_of(k), :], x_s, x_r.at[k],
+                    copy(g_new.at[rows_of(k), :], g_all.at[m, rows_of(k), :], x_s, c_r.at[0, k],
                          {"section": s + 1}).wait_recv()
 
                 for j, q in enumerate(others(chip, chips)):
@@ -781,7 +781,7 @@
                 dma, dma((away, PIECES)),
                 dma, dma((n_sec - 1, PIECES)),
                 dma, dma((away, PIECES)), dma((chips, PIECES // GROUP)),
-                dma, dma((PIECES,)),
+                dma,
                 dma, dma((away,)), dma((chips,)),
                 dma, dma,
                 dma, dma((2, 3 if n_dp == 4 else n_dp)), dma((2, 2, 2)), dma, dma,

time: 62.5 us -> 62.4 us (level)
  no operation moved by 1% of the time
where the time goes in v6:
time: 62.4 us; the launch traced here: 62.3 us
  Pallas kernels  61 us (98%)
  between operations  1.29 us (2%)
    pallas_call x1, Pallas kernels, body(): pl.pallas_call(make_kernel(n_sec, n_dp, n_mp), out_shape=(pltpu.VMEM((own...  59.9 us

profile of v6, /device:TPU:9, one launch (start us, length us, event | category | flops | bytes accessed | tf_op | source)
XLA Modules:
  0.0 62.3 jit_solution(5871942377065707452)
XLA Ops:
  1.3 59.9 %shard_map.93 = (bf16[256,512]{1,0:T(8,128)(2,1)S(1)}, bf16[1024,256]{1,0:T(8,128)(2,1)S(1)}, f32[128,512]{1,0:T(8,128)S(1)}, f32[128,512]{1,0:T(8,128)S(1)}) custom-call(bf16[1024,512]{1,0:T(8,128)(2,1)} %text_in.1, bf16[256,512]{1,0:T(8,128)(2,1)} %image_in.1, f32[1]{0:T(128)S(6)} %copy.10.scale_ref, bf16[1024,512]{1,0:T(8,128)(2,1)} %bitcast.3, ...), custom_call_target="tpu_custom_call" | custom-call | tf_op jit(solution)/shard_map/pallas_call | solution.py:724
  61.2 1.1 %shard_map.94 = (bf16[256,512]{1,0:T(8,128)(2,1)}, bf16[1024,256]{1,0:T(8,128)(2,1)}, f32[1,128,512]{2,1,0:T(8,128)}, f32[1,128,512]{2,1,0:T(8,128)}) custom-call(bf16[256,512]{1,0:T(8,128)(2,1)S(1)} %get-tuple-element.8.image, bf16[1024,256]{1,0:T(8,128)(2,1)S(1)} %get-tuple-element.9.inputs, f32[128,512]{1,0:T(8,128)S(1)} %get-tuple-element.10.first, ...), custom_call_target="tpu_custom_call" | custom-call | tf_op jit(solution)/shard_map/pallas_call | solution.py:797
